TPU v7x, 128 devices: a whole 4x4x4 slice. The times are simulated.
128 devices in a mesh: ka: 32 (over z, y, core), col: 4 (over x).
Axes of the slice: x: 4, y: 4, z: 4, core: 2. Of those that a mesh axis runs over, the one named last changes fastest.
Arguments:
- hamiltonian: bfloat16 [1024, 2, 9216], P(('ka', 'col')), may hold values from -0.1875 to 0.1875
- eigvecs: bfloat16 [2048, 2, 96, 96], P('ka'), may hold values from -0.625 to 0.625
- spin: bfloat16 [2, 96, 96], replicated, may hold values from -0.059814453 to 0.059814453
- k_indices: int32 [2048, 3], P('ka'), may hold values from 0 to 63
- r_vectors: int32 [1024, 3], replicated, may hold values from -5 to 5, as said below
- degeneracy: int32 [1024], replicated, may hold values from 1 to 4
- fermi_level: float32 [1], replicated, may hold values from -0.5 to 0.5
Outputs:
- band_curvature: float32 [9, 96, 2048], P(None, None, ('ka', 'col'))
- conductivity: float32 [9, 96], replicated
Inputs may be any that keep to these rules, and one draw needn't show every extreme that they name: `r_vectors`: the 1024 lattice vectors are all distinct.
All inputs are finite; a program needn't handle non-finite values.
Results may differ from a plain program's by a relative error of at most 0.0085.
The roundings to bfloat16 on the way count: a program that leaves them out, or rounds other values in their place, can miss the bound.
Values may be sent and summed in bfloat16 or wider, within the bound.
No kernel may reach another device: no remote copies, remote signals or barrier semaphores. Data moves between devices by JAX's collectives and lax.ppermute only.
A program may use at most 128 MiB of HBM per device.

v0:
```python
import math

import jax
import jax.numpy as jnp
from jax import lax
from jax.sharding import PartitionSpec as P

WF = 96
GRID = 64


two_pi = 2.0 * math.pi
broadening = 0.5
smearing = 0.1


def sent_to_all(value, axis):
    copies = jnp.broadcast_to(value, (lax.axis_size(axis), *value.shape))
    return lax.all_to_all(copies, axis, split_axis=0, concat_axis=0, tiled=True)


def taken_together(value, axis):
    everything = sent_to_all(value, axis)
    return jnp.sum(everything, axis=0)


def phase_rows(kpoints, lattice, degrees, height):
    flat_index = jnp.arange(height, dtype=jnp.int32)
    vector_index = flat_index // 2
    halves = flat_index % 2
    lattice_rows = jnp.take(lattice, vector_index, axis=0)
    degree_rows = jnp.take(degrees, vector_index, axis=0)
    lattice_dot = jnp.mod(jnp.sum(kpoints[:, None, :] * lattice_rows[None, :, :], axis=-1), GRID)
    angles = lattice_dot.astype(jnp.float32) * (two_pi / GRID)
    cosine = jnp.cos(angles)
    sine_part = jnp.sin(angles)
    inverse = 1.0 / degree_rows.astype(jnp.float32)
    coords = lattice_rows.astype(jnp.float32) * inverse[:, None]
    real_part = jnp.stack(
        [
            cosine * inverse,
            -sine_part * coords[:, 0],
            -sine_part * coords[:, 1],
            -sine_part * coords[:, 2],
        ],
        axis=1,
    )
    imag_part = jnp.stack(
        [sine_part * inverse, cosine * coords[:, 0], cosine * coords[:, 1], cosine * coords[:, 2]],
        axis=1,
    )
    real_rows = (halves == 0)[None, None, :]
    top_rows = jnp.where(real_rows, real_part, -imag_part)
    low_rows = jnp.where(real_rows, imag_part, real_part)
    return jnp.stack([top_rows, low_rows], axis=2)


def rotate(operators, vectors):
    ops_re = operators[:, :, 0]
    ops_im = operators[:, :, 1]
    vec_re = vectors[:, 0]
    vec_im = vectors[:, 1]
    half_re = jnp.einsum(
        "kcij,kjm->kcim", ops_re, vec_re, preferred_element_type=jnp.float32
    ) - jnp.einsum("kcij,kjm->kcim", ops_im, vec_im, preferred_element_type=jnp.float32)
    half_im = jnp.einsum(
        "kcij,kjm->kcim", ops_re, vec_im, preferred_element_type=jnp.float32
    ) + jnp.einsum("kcij,kjm->kcim", ops_im, vec_re, preferred_element_type=jnp.float32)
    half_re = half_re.astype(jnp.bfloat16)
    half_im = half_im.astype(jnp.bfloat16)
    full_re = jnp.einsum(
        "kjn,kcjm->kcnm", vec_re, half_re, preferred_element_type=jnp.float32
    ) + jnp.einsum("kjn,kcjm->kcnm", vec_im, half_im, preferred_element_type=jnp.float32)
    full_im = jnp.einsum(
        "kjn,kcjm->kcnm", vec_re, half_im, preferred_element_type=jnp.float32
    ) - jnp.einsum("kjn,kcjm->kcnm", vec_im, half_re, preferred_element_type=jnp.float32)
    sym_re = (full_re + jnp.swapaxes(full_re, -1, -2)) * 0.5
    sym_im = (full_im - jnp.swapaxes(full_im, -1, -2)) * 0.5
    return jnp.stack([sym_re, sym_im], axis=2).astype(jnp.bfloat16)


def kubo(bloch_ops, spin_bloch, fermi_level):
    energy = jnp.diagonal(bloch_ops[:, 0, 0].astype(jnp.float32), axis1=-2, axis2=-1)
    velo_re = bloch_ops[:, 1:, 0].astype(jnp.float32)
    velo_im = bloch_ops[:, 1:, 1].astype(jnp.float32)
    spin_re = spin_bloch[:, 0].astype(jnp.float32)
    spin_im = spin_bloch[:, 1].astype(jnp.float32)
    prod_re = jnp.einsum("kij,kajm->kaim", spin_re, velo_re) - jnp.einsum(
        "kij,kajm->kaim", spin_im, velo_im
    )
    prod_im = jnp.einsum("kij,kajm->kaim", spin_re, velo_im) + jnp.einsum(
        "kij,kajm->kaim", spin_im, velo_re
    )
    cur_re = (prod_re + jnp.swapaxes(prod_re, -1, -2)) * 0.5
    cur_im = (prod_im - jnp.swapaxes(prod_im, -1, -2)) * 0.5
    energy_gap = energy[:, :, None] - energy[:, None, :]
    weight = 1.0 / (energy_gap * energy_gap + broadening * broadening)
    curvature = -2.0 * (
        jnp.einsum("kanm,kbmn,knm->kabn", cur_re, velo_im, weight)
        + jnp.einsum("kanm,kbmn,knm->kabn", cur_im, velo_re, weight)
    )
    occupation = 1.0 / (1.0 + jnp.exp((energy - fermi_level[0]) / smearing))
    weighted = jnp.einsum("kn,kabn->abn", occupation, curvature)
    return (curvature, weighted)


def on_device(hamiltonian, eigvecs, spin, k_indices, r_vectors, degeneracy, fermi_level):
    kcount = eigvecs.shape[0]
    col_count = lax.axis_size("col")
    quarter = kcount // col_count
    column = lax.axis_index("col")
    vectors = lax.dynamic_slice_in_dim(eigvecs, column * quarter, quarter, 0)
    flat_shard = hamiltonian.reshape(hamiltonian.shape[0] * 2, WF * WF)
    entry_width = WF * WF // col_count
    entry_slice = lax.all_to_all(flat_shard, "col", split_axis=1, concat_axis=0, tiled=True)
    segment = lax.all_gather(entry_slice, "ka", axis=0, tiled=True)
    height = segment.shape[0]
    phases = phase_rows(k_indices, r_vectors, degeneracy, height)
    phases = phases.reshape(kcount * 8, height).astype(jnp.bfloat16)
    summed = jnp.dot(phases, segment, preferred_element_type=jnp.float32)
    summed = summed.reshape(kcount, 4, 2, entry_width)
    own_entries = summed.astype(jnp.bfloat16)
    regrouped = lax.all_to_all(own_entries, "col", split_axis=0, concat_axis=3, tiled=True)
    interpolated = regrouped.reshape(quarter, 4, 2, WF, WF)
    bloch_ops = rotate(interpolated, vectors)
    spin_wide = spin.astype(jnp.float32)
    spin_sym = jnp.stack(
        [(spin_wide[0] + spin_wide[0].T) * 0.5, (spin_wide[1] - spin_wide[1].T) * 0.5]
    ).astype(jnp.bfloat16)
    spin_ops = jnp.broadcast_to(spin_sym[None, None], (quarter, 1, 2, WF, WF))
    spin_bloch = rotate(spin_ops, vectors)[:, 0]
    curvature, weighted = kubo(bloch_ops, spin_bloch, fermi_level)
    total_points = kcount * lax.axis_size("ka")
    partial_value = weighted.reshape(9, WF) / math.sqrt(total_points)
    totals = taken_together(taken_together(partial_value, "col"), "ka")
    band_out = jnp.transpose(curvature, (1, 2, 3, 0)).reshape(9, WF, quarter)
    return (band_out, totals)


def solution(mesh):
    in_specs = (
        P(("ka", "col"), None, None),
        P("ka", None, None, None),
        P(),
        P("ka", None),
        P(),
        P(),
        P(),
    )
    out_specs = (P(None, None, ("ka", "col")), P())
    return jax.shard_map(
        on_device, mesh=mesh, in_specs=in_specs, out_specs=out_specs, check_vma=False
    )
```

profile of v0, /device:TPU:1, one launch (start us, length us, event | category | flops | bytes accessed | tf_op | source)
XLA Modules:
  0.0 234.4 jit_solution(3155142561728896138)
XLA Ops:
  8.6 10.6 %all_to_all.44 = bf16[16,4,2304]{2,0,1:T(8,128)(2,1)} all-to-all(bf16[16,4,2304]{2,0,1:T(8,128)(2,1)S(1)} %copy.186), channel_id=1, replica_groups=mesh['ka'=32,'col'=4] {'col'}, dimensions={1} | all-to-all | bytes 589824 | tf_op jit(solution)/shard_map/all_to_all | solution.py:115
  22.6 8.6 %gather_fusion.1 = s32[2048]{0:T(1024)S(1)} fusion(s32[1024]{0:T(1024)S(1)} %copy-done.2, s32[2048]{0:T(1024)S(1)} %broadcast_clamp_fusion), kind=kCustom, calls=%fused_computation.1 | custom fusion | bytes 24576 | tf_op jit(solution)/shard_map/jit(_take)/gather | solution.py:32
  31.1 8.6 %gather_fusion = s32[2048,3]{1,0:T(8,128)} fusion(s32[1024,3]{1,0:T(8,128)} %copy.184, s32[2048]{0:T(1024)S(1)} %broadcast_clamp_fusion), kind=kCustom, calls=%fused_computation | custom fusion | bytes 57344 | tf_op jit(solution)/shard_map/jit(_take)/gather | solution.py:31
  39.8 2.7 %convert_multiply_fusion = (f32[2048,3]{1,0:T(8,128)}, s32[2048,3]{1,0:T(8,128)}) fusion(f32[2048]{0:T(1024)S(1)} %convert_divide_fusion, s32[2048,3]{1,0:T(8,128)} %gather_fusion, pred[2048]{0:T(1024)(128)(4,1)S(1)} %fusion.93), kind=kLoop, calls=%fused_computation.55 | loop fusion | flops 18432 | bytes 83968 | tf_op jit(solution)/shard_map/mul | solution.py:38
  44.5 3.5 %slice_reduce_fusion.2 = (f32[2048]{0:T(1024)S(1)}, f32[2048]{0:T(1024)S(1)}, f32[2048]{0:T(1024)S(1)}) fusion(f32[2048,3]{1,0:T(8,128)} %get-tuple-element.5), kind=kLoop, calls=%fused_computation.54 | loop fusion | bytes 49152 | tf_op jit(solution)/shard_map/slice | solution.py:42
  56.1 20.9 %all-gather.2.cloned.1.call-done = bf16[2048,2304]{1,0:T(8,128)(2,1)} async-done(((bf16[64,2304]{1,0:T(8,128)(2,1)}), bf16[2048,2304]{1,0:T(8,128)(2,1)}) %all-gather.2.cloned.1.call-update) | async-done | bytes 9437200 | tf_op jit(solution)/shard_map/all_gather | solution.py:116
  77.1 9.3 %fusion.2 = bf16[64,4,2,2304]{3,0,2,1:T(8,128)(2,1)S(1)} fusion(bf16[2048,2304]{1,0:T(8,128)(2,1)} %all-gather.2.cloned.1.call-done, bf16[64,4,1,2048]{3,0,2,1:T(8,128)(2,1)} %get-tuple-element.8, bf16[64,4,1,2048]{3,0,2,1:T(8,128)(2,1)} %get-tuple-element.7), kind=kOutput, calls=%fused_computation.5 | convolution fusion | flops 4834066432 | bytes 13893632 | tf_op jit(solution)/shard_map/dot_general | solution.py:120
  86.4 3.8 %copy.187 = bf16[64,4,2,2304]{3,2,1,0:T(2,128)(2,1)} copy(bf16[64,4,2,2304]{3,0,2,1:T(8,128)(2,1)S(1)} %fusion.2) | data formatting | bytes 4718592 | tf_op jit(solution)/shard_map/convert_element_type | solution.py:122
  90.2 4.7 %all-to-all-start.1 = ((bf16[64,4,2,2304]{3,2,1,0:T(2,128)(2,1)}), bf16[64,4,2,2304]{3,2,1,0:T(2,128)(2,1)}, u32[]{:S(2)}, u32[]{:S(2)}) async-start(bf16[64,4,2,2304]{3,2,1,0:T(2,128)(2,1)} %copy.187), calls=%async_computation.1 | async-start | bytes 4718592 | tf_op jit(solution)/shard_map/all_to_all | solution.py:123
  99.0 2.3 copy.203
  103.8 2.3 copy.207
  106.9 2.2 fusion.34
  109.2 14.5 %all-to-all-done.1 = bf16[64,4,2,2304]{3,2,1,0:T(2,128)(2,1)} async-done(((bf16[64,4,2,2304]{3,2,1,0:T(2,128)(2,1)}), bf16[64,4,2,2304]{3,2,1,0:T(2,128)(2,1)}, u32[]{:S(2)}, u32[]{:S(2)}) %all-to-all-start.1) | async-done | bytes 2359328 | tf_op jit(solution)/shard_map/all_to_all | solution.py:123
  123.7 5.0 %copy.260 = bf16[4,16,4,2,2304]{4,0,2,1,3:T(4,128)(2,1)} copy(bf16[4,16,4,2,2304]{4,3,2,1,0:T(2,128)(2,1)} %bitcast.16) | data formatting | bytes 4718592 | tf_op jit(solution)/shard_map/all_to_all | solution.py:123
  128.7 7.4 %reshape.803 = bf16[16,4,2,96,96]{4,3,1,0,2:T(8,128)(2,1)} reshape(bf16[16,4,2,4,2304]{4,3,1,0,2:T(4,128)(2,1)} %bitcast.234) | data formatting | bytes 4718592 | tf_op jit(solution)/shard_map/reshape | solution.py:124
  141.4 2.3 fusion.49
  143.6 2.3 convolution_subtract_fusion
  145.9 3.6 %copy.192 = f32[16,4,96,96]{2,3,1,0:T(8,128)} copy(f32[16,4,96,96]{3,2,1,0:T(8,128)} %convolution_subtract_fusion) | data formatting | bytes 4718592 | tf_op jit(solution)/shard_map/sub | solution.py:74
  149.5 4.7 %convolution_add_fusion = f32[16,4,96,96]{3,2,1,0:T(8,128)} fusion(f32[16,4,96,96]{3,2,1,0:T(8,128)} %fusion.49, bf16[16,4,96,96]{3,2,1,0:T(8,128)(2,1)} %copy-done.10, bf16[64,2,96,96]{3,2,1,0:T(8,128)(2,1)S(1)} %copy-done, s32[]{:T(128)S(6)} %select_n.239, s32[]{:T(128)S(6)} %add.272), kind=kOutput, calls=%fused_computation.32 | convolution fusion | flops 113836032 | bytes 6291464 | tf_op jit(solution)/shard_map/kjn,kcjm->kcnm/dot_general | solution.py:73
  154.1 3.8 %copy.195 = f32[16,4,96,96]{3,2,1,0:T(8,128)} copy(f32[16,4,96,96]{2,3,1,0:T(8,128)} %bitcast.232) | data formatting | bytes 4718592 | tf_op jit(solution)/shard_map/add | solution.py:71
  157.9 5.3 %fusion.18 = (bf16[16,4,1,96,96]{4,3,1,0,2:T(8,128)(2,1)S(1)}, bf16[16,4,1,96,96]{4,3,1,0,2:T(8,128)(2,1)S(1)}) fusion(f32[16,4,96,96]{3,2,1,0:T(8,128)} %copy.195, f32[16,4,96,96]{3,2,1,0:T(8,128)} %convolution_add_fusion, f32[16,4,96,96]{3,2,1,0:T(8,128)S(1)} %copy-done.3, f32[16,4,96,96]{2,3,1,0:T(8,128)} %copy.192), kind=kLoop, calls=%fused_computation.36 | loop fusion | flops 3538944 | bytes 11796480 | tf_op jit(solution)/shard_map/stack | solution.py:79
  169.3 3.3 %fusion.12 = bf16[16,3,96,96]{3,2,1,0:T(8,128)(2,1)} fusion(f32[16,3,96,96]{3,2,1,0:T(8,128)S(1)} %convolution_subtract_fusion.1, f32[16,3,96,96]{2,3,1,0:T(8,128)} %copy.209), kind=kLoop, calls=%fused_computation.21 | loop fusion | flops 1327104 | bytes 4423680 | tf_op jit(solution)/shard_map/mul | solution.py:94
  175.2 3.1 %subtract_multiply_fusion = bf16[16,3,96,96]{3,2,1,0:T(8,128)(2,1)} fusion(f32[16,3,96,96]{3,2,1,0:T(8,128)} %copy.214, f32[16,3,96,96]{3,2,1,0:T(8,128)S(1)} %convolution_add_fusion.1), kind=kLoop, calls=%fused_computation.24 | loop fusion | flops 1327104 | bytes 4423680 | tf_op jit(solution)/shard_map/mul | solution.py:95
  178.3 4.0 %copy.196 = f32[16,96,96]{0,2,1:T(8,128)} copy(f32[16,96,96]{2,1,0:T(8,128)} %fusion.36) | data formatting | bytes 1179648 | tf_op jit(solution)/shard_map/convert_element_type | solution.py:83
  182.2 3.0 %gather_fusion.2 = f32[96,16]{1,0:T(8,128)S(1)} fusion(f32[16,96,96]{0,2,1:T(8,128)} %copy.196, s32[96]{0:T(128)S(1)} %or_bitcast_fusion), kind=kCustom, calls=%fused_computation.2 | custom fusion | bytes 13056 | tf_op jit(solution)/shard_map/jit(diagonal)/gather | solution.py:83
  187.5 2.8 %copy.215 = bf16[16,96,96,3]{2,3,1,0:T(4,128)(2,1)S(1)} copy(bf16[16,96,96,3]{1,2,3,0:T(8,128)(2,1)} %get-tuple-element.10) | data formatting | bytes 1769472 | tf_op jit(solution)/shard_map/kanm,kbmn,knm->kabn/dot_general | solution.py:100
  190.4 3.9 %copy.210 = bf16[16,96,96,3]{2,3,1,0:T(4,128)(2,1)} copy(bf16[16,96,96,3]{1,2,3,0:T(8,128)(2,1)} %get-tuple-element.9) | data formatting | bytes 1769472 | tf_op jit(solution)/shard_map/kanm,kbmn,knm->kabn/dot_general | solution.py:99
  196.1 5.7 %fusion.5 = (f32[96,3,3]{1,2,0:T(4,128)S(1)}, f32[16,96,3,3]{3,2,1,0:T(4,128)}) fusion(f32[96,16]{0,1:T(8,128)S(1)} %divide_bitcast_fusion, f32[16,96,3,3]{3,2,1,0:T(4,128)S(1)} %fusion.8, bf16[16,96,96,3]{2,3,1,0:T(4,128)(2,1)S(1)} %copy-done.18, bf16[16,3,96,96]{3,2,1,0:T(8,128)(2,1)S(1)} %copy-done.19), kind=kOutput, calls=%fused_computation.7 | convolution fusion | flops 2708640 | bytes 1889664 | tf_op jit(solution)/shard_map/kanm,kbmn,knm->kabn/dot_general | solution.py:99
  202.0 6.5 %all_to_all.45 = f32[4,1,864]{2,1,0:T(1,128)S(1)} all-to-all(f32[4,1,864]{2,1,0:T(1,128)S(1)} %reshape.838), channel_id=1, replica_groups=mesh['ka'=32,'col'=4] {'col'}, dimensions={0} | all-to-all | bytes 27648 | tf_op jit(solution)/shard_map/all_to_all | solution.py:19
  210.7 7.7 %all-to-all-start.3 = ((f32[32,1,864]{2,1,0:T(1,128)}), f32[32,1,864]{2,1,0:T(1,128)S(1)}, u32[]{:S(2)}, u32[]{:S(2)}) async-start(f32[32,1,864]{2,1,0:T(1,128)} %reshape.840), calls=%async_computation.3 | async-start | bytes 229376 | tf_op jit(solution)/shard_map/all_to_all | solution.py:19
  218.4 2.9 %copy.217 = f32[3,3,96,16]{2,3,1,0:T(8,128)} copy(f32[3,3,96,16]{0,1,2,3:T(4,128)} %bitcast.236) | data formatting | bytes 110592 | tf_op jit(solution)/shard_map/mul | solution.py:98
  221.3 4.6 %all-to-all-done.3 = f32[32,1,864]{2,1,0:T(1,128)S(1)} async-done(((f32[32,1,864]{2,1,0:T(1,128)}), f32[32,1,864]{2,1,0:T(1,128)S(1)}, u32[]{:S(2)}, u32[]{:S(2)}) %all-to-all-start.3) | async-done | bytes 110624 | tf_op jit(solution)/shard_map/all_to_all | solution.py:19
  (108 shorter events, 43.3 us)
Async XLA Ops:
  7.2 40.9 %copy-start = (bf16[64,2,96,96]{3,2,1,0:T(8,128)(2,1)S(1)}, bf16[64,2,96,96]{3,2,1,0:T(8,128)(2,1)}, u32[]{:S(2)}) copy-start(bf16[64,2,96,96]{3,2,1,0:T(8,128)(2,1)} %param.8) | copy-start | bytes 7077892
  7.2 15.4 %copy-start.2 = (s32[1024]{0:T(1024)S(1)}, s32[1024]{0:T(1024)}, u32[]{:S(2)}) copy-start(s32[1024]{0:T(1024)} %param.12) | copy-start | bytes 12292
  7.2 69.9 %all-gather.2.cloned.1.call-start = ((), (), s32[]{:S(2)}) async-start(), calls=%async_computation.4 | async-start | bytes 9732096 | tf_op jit(solution)/shard_map/all_gather | solution.py:116
  39.8 4.5 %copy-start.22 = (s32[64,3]{0,1:T(4,128)S(1)}, s32[64,3]{0,1:T(4,128)}, u32[]{:S(2)}) copy-start(s32[64,3]{0,1:T(4,128)} %param.10) | copy-start | bytes 2308
  48.0 0.6 copy-start.21
  48.0 4.3 %copy-start.20 = (bf16[96,96]{1,0:T(8,128)(2,1)}, bf16[96,96]{1,0:T(8,128)(2,1)S(1)}, u32[]{:S(2)}) copy-start(bf16[96,96]{1,0:T(8,128)(2,1)S(1)} %get-tuple-element.19) | copy-start | bytes 55300
  90.2 33.5 %all-to-all-start.1 = ((bf16[64,4,2,2304]{3,2,1,0:T(2,128)(2,1)}), bf16[64,4,2,2304]{3,2,1,0:T(2,128)(2,1)}, u32[]{:S(2)}, u32[]{:S(2)}) async-start(bf16[64,4,2,2304]{3,2,1,0:T(2,128)(2,1)} %copy.187), calls=%async_computation.1 | async-start | bytes 4718592 | tf_op jit(solution)/shard_map/all_to_all | solution.py:123
  94.9 2.9 %copy-start.16 = (f32[16,96,96]{2,1,0:T(8,128)S(1)}, f32[16,96,96]{2,1,0:T(8,128)}, u32[]{:S(2)}) copy-start(f32[16,96,96]{2,1,0:T(8,128)} %fusion.42) | copy-start | bytes 1769476
  97.0 0.8 copy-start.14
  106.1 3.0 %copy-start.12 = (f32[16,96,96]{2,1,0:T(8,128)S(1)}, f32[16,96,96]{2,1,0:T(8,128)}, u32[]{:S(2)}) copy-start(f32[16,96,96]{2,1,0:T(8,128)} %convolution_subtract_fusion.2) | copy-start | bytes 1769476
  106.1 3.0 %copy-start.17 = (f32[16,1,96,96]{3,2,0,1:T(8,128)S(1)}, f32[16,1,96,96]{3,2,0,1:T(8,128)}, u32[]{:S(2)}) copy-start(f32[16,1,96,96]{3,2,0,1:T(8,128)} %copy.207) | copy-start | bytes 1769476
  136.1 2.4 %copy-start.4 = (bf16[16,4,2,96,96]{4,3,1,0,2:T(8,128)(2,1)S(1)}, bf16[16,4,2,96,96]{4,3,1,0,2:T(8,128)(2,1)}, u32[]{:S(2)}) copy-start(bf16[16,4,2,96,96]{4,3,1,0,2:T(8,128)(2,1)} %reshape.803) | copy-start | bytes 7077892
  139.6 1.1 copy-start.10
  154.1 3.8 %copy-start.3 = (f32[16,4,96,96]{3,2,1,0:T(8,128)S(1)}, f32[16,4,96,96]{3,2,1,0:T(8,128)}, u32[]{:S(2)}) copy-start(f32[16,4,96,96]{3,2,1,0:T(8,128)} %convolution_subtract_fusion) | copy-start | bytes 7077892
  157.9 6.4 %copy-start.15 = (bf16[16,96,96,1]{2,1,3,0:T(8,128)(2,1)S(1)}, bf16[16,96,96,1]{2,1,3,0:T(8,128)(2,1)}, u32[]{:S(2)}) copy-start(bf16[16,96,96,1]{2,1,3,0:T(8,128)(2,1)} %fusion.34) | copy-start | bytes 884740
  163.2 1.6 copy-start.5
  163.2 3.6 %copy-start.8 = (bf16[16,4,1,96,96]{4,3,1,0,2:T(8,128)(2,1)}, bf16[16,4,1,96,96]{4,3,1,0,2:T(8,128)(2,1)S(1)}, u32[]{:S(2)}) copy-start(bf16[16,4,1,96,96]{4,3,1,0,2:T(8,128)(2,1)S(1)} %get-tuple-element.24) | copy-start | bytes 3538948
  169.3 3.4 %copy-start.6 = (bf16[16,4,1,96,96]{4,3,1,0,2:T(8,128)(2,1)S(1)}, bf16[16,4,1,96,96]{4,3,1,0,2:T(8,128)(2,1)}, u32[]{:S(2)}) copy-start(bf16[16,4,1,96,96]{4,3,1,0,2:T(8,128)(2,1)} %copy-done.5) | copy-start | bytes 3538948
  169.3 3.4 %copy-start.11 = (f32[16,3,96,96]{3,2,1,0:T(8,128)S(1)}, f32[16,3,96,96]{3,2,1,0:T(8,128)}, u32[]{:S(2)}) copy-start(f32[16,3,96,96]{3,2,1,0:T(8,128)} %fusion.25) | copy-start | bytes 5308420
  178.3 7.3 %copy-start.7 = (bf16[16,4,1,96,96]{4,3,1,0,2:T(8,128)(2,1)S(1)}, bf16[16,4,1,96,96]{4,3,1,0,2:T(8,128)(2,1)}, u32[]{:S(2)}) copy-start(bf16[16,4,1,96,96]{4,3,1,0,2:T(8,128)(2,1)} %copy-done.5) | copy-start | bytes 3538948
  178.3 7.3 %copy-start.9 = (bf16[16,4,1,96,96]{4,3,1,0,2:T(8,128)(2,1)S(1)}, bf16[16,4,1,96,96]{4,3,1,0,2:T(8,128)(2,1)}, u32[]{:S(2)}) copy-start(bf16[16,4,1,96,96]{4,3,1,0,2:T(8,128)(2,1)} %copy-done.8) | copy-start | bytes 3538948
  187.5 6.7 %copy-start.13 = (bf16[16,3,96,96]{3,2,1,0:T(8,128)(2,1)S(1)}, bf16[16,3,96,96]{3,2,1,0:T(8,128)(2,1)}, u32[]{:S(2)}) copy-start(bf16[16,3,96,96]{3,2,1,0:T(8,128)(2,1)} %subtract_multiply_fusion) | copy-start | bytes 2654212
  194.3 1.8 copy-start.18
  194.3 1.8 copy-start.19
  209.9 17.7 %copy-start.1 = (bf16[64,2,96,96]{3,2,1,0:T(8,128)(2,1)S(1)}, bf16[64,2,96,96]{3,2,1,0:T(8,128)(2,1)}, u32[]{:S(2)}) copy-start(bf16[64,2,96,96]{3,2,1,0:T(8,128)(2,1)} %param.8) | copy-start | bytes 7077892
  210.7 15.1 %all-to-all-start.3 = ((f32[32,1,864]{2,1,0:T(1,128)}), f32[32,1,864]{2,1,0:T(1,128)S(1)}, u32[]{:S(2)}, u32[]{:S(2)}) async-start(f32[32,1,864]{2,1,0:T(1,128)} %reshape.840), calls=%async_computation.3 | async-start | bytes 229376 | tf_op jit(solution)/shard_map/all_to_all | solution.py:19
Sparse Core Ops, SparseCore 0:
  19.3 57.7 all-gather.1
where the time goes:
time: 236 us; the launch traced here: 234 us
  local copies, waits for them, and re-layouts  78.6 us (33%)
  matrix products  41.4 us (18%)
  waiting for transfers between devices  40.1 us (17%)
  other arithmetic  29.5 us (12%)
  blocking collectives  17.1 us (7%)
  between operations  15.3 us (6%)
  starting transfers between devices  12.4 us (5%)
    all_gather x1, waiting for transfers between devices, on_device(): segment = lax.all_gather(entry_slice, 'ka', axis=0, tiled=True)  20.9 us
    all_to_all x1, waiting for transfers between devices, on_device(): lax.all_to_all(own_entries, 'col', split_axis=0, concat_axis=3, tiled=True)  14.5 us
    all_to_all x1, blocking collectives, on_device(): lax.all_to_all(flat_shard, 'col', split_axis=1, concat_axis=0, tiled=True)  10.6 us
    dot_general x1, matrix products, on_device(): summed = jnp.dot(phases, segment, preferred_element_type=jnp.float32)  9.27 us
    gather x1, local copies, waits for them, and re-layouts, phase_rows(): lattice_rows = jnp.take(lattice, vector_index, axis=0)  8.64 us
    gather x1, local copies, waits for them, and re-layouts, phase_rows(): degree_rows = jnp.take(degrees, vector_index, axis=0)  8.58 us
    all_to_all x1, starting transfers between devices, sent_to_all(): return lax.all_to_all(copies, axis, split_axis=0, concat_axis=0, tiled=True)  7.66 us
    reshape x1, local copies, waits for them, and re-layouts, on_device(): interpolated = regrouped.reshape(quarter, 4, 2, WF, WF)  7.42 us
  transfers between devices with their start and end apart: 3, of which 3 were waited for; matrix products, arithmetic and copies ran while one was open for 22% of the time, Pallas kernels for 0%

commit v1 on v0

v1 whole, which is shorter than its diff:
```python
import math

import jax
import jax.numpy as jnp
from jax import lax
from jax.experimental import pallas as pl
from jax.experimental.pallas import tpu as pltpu
from jax.sharding import Mesh, PartitionSpec as P

WF = 96
GRID = 64
NR = 1024
GROUP = 32
ROWS = 3
PIECE = ROWS * 2 * WF
WIDE = 640
KEPT = 4 * PIECE
QUARTER = 16
STEP_K = 128
PER_STEP = 2

two_pi = 2.0 * math.pi
broadening = 0.5
smearing = 0.1

ALL = ("z", "y", "core", "x")
PLANE = ("y", "core", "x")

f32 = jnp.float32
bf16 = jnp.bfloat16


def half_turn(count):
    y = count * (math.pi / GRID)
    q = y * y
    s = 1.0 - q * (1.0 / 110.0)
    s = 1.0 - q * (1.0 / 72.0) * s
    s = 1.0 - q * (1.0 / 42.0) * s
    s = 1.0 - q * (1.0 / 20.0) * s
    s = 1.0 - q * (1.0 / 6.0) * s
    s = y * s
    c = 1.0 - q * (1.0 / 132.0)
    c = 1.0 - q * (1.0 / 90.0) * c
    c = 1.0 - q * (1.0 / 56.0) * c
    c = 1.0 - q * (1.0 / 30.0) * c
    c = 1.0 - q * (1.0 / 12.0) * c
    c = 1.0 - q * (1.0 / 2.0) * c
    return 1.0 - 2.0 * s * s, 2.0 * s * c


def interpolate_kernel(k_ref, lat_ref, hop_ref, out_ref, w_ref, p_ref):
    @pl.when(pl.program_id(0) == 0)
    def _():
        lane = lax.broadcasted_iota(jnp.int32, (NR, 128), 1)
        tiles = [hop_ref[:, 128 * t : 128 * (t + 1)].astype(f32) for t in range(5)]
        tiles[4] = jnp.where(lane < 64, tiles[4], 0.0)
        ups = [pltpu.roll(t, 96, 1) for t in tiles]
        downs = [pltpu.roll(t, 32, 1) for t in tiles]
        for t in range(5):
            w_ref[0:NR, 128 * t : 128 * (t + 1)] = tiles[t].astype(bf16)
            before = ups[(t - 1) % 5]
            after = downs[(t + 1) % 5]
            up = jnp.where(lane < 96, before, ups[t])
            down = jnp.where(lane < 32, downs[t], after)
            place = (lane + 128 * t) % (2 * WF)
            turned = jnp.where(place < WF, -down, up)
            if t == 4:
                turned = jnp.where(lane < 64, turned, 0.0)
            w_ref[NR : 2 * NR, 128 * t : 128 * (t + 1)] = turned.astype(bf16)

    k = k_ref[...]
    r0 = lat_ref[0:1, :]
    r1 = lat_ref[1:2, :]
    r2 = lat_ref[2:3, :]
    inverse = 1.0 / lat_ref[3:4, :]
    dots = k[:, 0:1] * r0 + k[:, 1:2] * r1 + k[:, 2:3] * r2
    count = dots - 64.0 * jnp.floor(dots * (1.0 / 64.0) + 0.5)
    cosine, sine = half_turn(count)
    coords = [r0 * inverse, r1 * inverse, r2 * inverse]
    for c in range(4):
        rows = slice(c * STEP_K, (c + 1) * STEP_K)
        if c == 0:
            re, im = cosine * inverse, sine * inverse
        else:
            re, im = -sine * coords[c - 1], cosine * coords[c - 1]
        p_ref[rows, 0:NR] = re.astype(bf16)
        p_ref[rows, NR : 2 * NR] = im.astype(bf16)
    summed = jnp.dot(p_ref[...], w_ref[...], preferred_element_type=f32)
    lane = lax.broadcasted_iota(jnp.int32, (STEP_K, 128), 1)
    for pair in range(2):
        even = summed[2 * pair * STEP_K : (2 * pair + 1) * STEP_K]
        odd = summed[(2 * pair + 1) * STEP_K : (2 * pair + 2) * STEP_K]
        shifted = [pltpu.roll(odd[:, 128 * t : 128 * (t + 1)], 64, 1) for t in range(5)]
        for t in range(9):
            if t < 4:
                tile = even[:, 128 * t : 128 * (t + 1)]
            elif t == 4:
                tile = jnp.where(lane < 64, even[:, 512:640], shifted[0])
            else:
                tile = jnp.where(lane < 64, shifted[t - 5], shifted[t - 4])
            at = pair * 2 * PIECE + 128 * t
            out_ref[:, :, at : at + 128] = tile.reshape(STEP_K // QUARTER, QUARTER, 128).astype(bf16)


def interpolate(k_rows, lattice, hopping):
    per = STEP_K // QUARTER
    return pl.pallas_call(
        interpolate_kernel,
        grid=(GROUP * QUARTER // STEP_K,),
        in_specs=[
            pl.BlockSpec((STEP_K, 8), lambda i: (i, 0)),
            pl.BlockSpec((8, NR), lambda i: (0, 0)),
            pl.BlockSpec((NR, WIDE), lambda i: (0, 0)),
        ],
        out_specs=pl.BlockSpec((per, QUARTER, KEPT), lambda i: (i, 0, 0)),
        out_shape=jax.ShapeDtypeStruct((GROUP, QUARTER, KEPT), bf16),
        scratch_shapes=[
            pltpu.VMEM((2 * NR, WIDE), bf16),
            pltpu.VMEM((4 * STEP_K, 2 * NR), bf16),
        ],
        compiler_params=pltpu.CompilerParams(
            dimension_semantics=("arbitrary",), vmem_limit_bytes=40 << 20
        ),
        name="interpolate",
    )(k_rows, lattice, hopping)


def flip(x):
    return jnp.transpose(x, (1, 0))


def bands_kernel(
    vec_ref, got_ref, spin_ref, fermi_ref, curve_ref, total_ref,
    wide_ref, we_ref, wo_ref, sp_ref, ut_ref, rh_ref, keep_ref, sum_ref,
):
    step = pl.program_id(0)

    @pl.when(step == 0)
    def _():
        for t in range(KEPT // 128):
            tile = got_ref[:, :, 128 * t : 128 * (t + 1)].astype(f32)
            wide_ref[t] = tile.reshape(GROUP * QUARTER, 128)
        we_ref[...] = jnp.zeros_like(we_ref)
        wo_ref[...] = jnp.zeros_like(wo_ref)
        ut_ref[...] = jnp.zeros_like(ut_ref)
        rh_ref[...] = jnp.zeros_like(rh_ref)
        sum_ref[...] = jnp.zeros_like(sum_ref)
        keep_ref[...] = jnp.zeros_like(keep_ref)
        sp_ref[...] = jnp.zeros_like(sp_ref)
        spin_re = spin_ref[0].astype(f32)
        spin_im = spin_ref[1].astype(f32)
        sym_re = (spin_re + flip(spin_re)) * 0.5
        sym_im = (spin_im - flip(spin_im)) * 0.5
        sp_ref[:, 0:WF] = sym_re.astype(bf16)
        sp_ref[:, WF : 2 * WF] = sym_im.astype(bf16)

    lane = lax.broadcasted_iota(jnp.int32, (WF, 128), 1)
    row = lax.broadcasted_iota(jnp.int32, (WF, 128), 0)
    eye = lane == row
    fermi = fermi_ref[0, 0]

    for q in range(PER_STEP):
        k = step * PER_STEP + q
        u_re = vec_ref[q, 0]
        u_im = vec_ref[q, 1]
        for ref, at in ((we_ref, 0), (wo_ref, 64)):
            ref[q, at : at + WF, 0:WF] = u_re
            ref[q, at : at + WF, 128 : 128 + WF] = u_im
            ref[q, at + WF : at + 2 * WF, 0:WF] = -u_im
            ref[q, at + WF : at + 2 * WF, 128 : 128 + WF] = u_re
        ut_ref[q, :, 0:WF] = flip(u_re.astype(f32)).astype(bf16)
        ut_ref[q, :, 128 : 128 + WF] = flip(u_im.astype(f32)).astype(bf16)

        def window(c, r):
            at = c * PIECE + r * 2 * WF
            first = at // 128
            parts = [
                wide_ref[first + j, pl.ds(k, GROUP, stride=QUARTER), :].astype(bf16)
                for j in range(2)
            ]
            return jnp.concatenate(parts, axis=1), at % 128 != 0

        groups = {False: [], True: []}
        where = {}
        for c in range(4):
            for r in range(ROWS):
                value, odd = window(c, r)
                where[c, r] = (odd, 32 * len(groups[odd]))
                groups[odd].append(value)
        even_rows = jnp.concatenate(groups[False] + [sp_ref[...]], axis=0)
        odd_rows = jnp.concatenate(groups[True], axis=0)
        halves = {
            False: jnp.dot(even_rows, we_ref[q], preferred_element_type=f32).astype(bf16),
            True: jnp.dot(odd_rows, wo_ref[q], preferred_element_type=f32).astype(bf16),
        }
        blochs = []
        for c in range(5):
            if c < 4:
                parts = []
                for r in range(ROWS):
                    odd, at = where[c, r]
                    parts.append(halves[odd][at : at + 32])
                half = jnp.concatenate(parts, axis=0)
            else:
                half = halves[False][192:288]
            h_re = half[:, 0:128]
            h_im = half[:, 128:256]
            rh_ref[q, c, 0:WF, 0:128] = h_re
            rh_ref[q, c, 0:WF, 128:256] = h_im
            rh_ref[q, c, 128 : 128 + WF, 0:128] = h_im
            rh_ref[q, c, 128 : 128 + WF, 128:256] = -h_re
            full = jnp.dot(ut_ref[q], rh_ref[q, c], preferred_element_type=f32)
            f_re = full[:, 0:128]
            f_im = full[:, 128:256]
            pad = jnp.zeros((32, 128), f32)
            t_re = flip(jnp.concatenate([f_re, pad], axis=0))[0:WF]
            t_im = flip(jnp.concatenate([f_im, pad], axis=0))[0:WF]
            b_re = ((f_re + t_re) * 0.5).astype(bf16)
            b_im = ((f_im - t_im) * 0.5).astype(bf16)
            blochs.append((b_re, b_im))
        diag = jnp.where(eye, blochs[0][0].astype(f32), 0.0)
        e_row = jnp.sum(diag, axis=0, keepdims=True)
        e_col = jnp.sum(diag, axis=1, keepdims=True)
        gap = e_col - e_row
        weight = -2.0 / (gap * gap + broadening * broadening)
        occupation = 1.0 / (1.0 + jnp.exp((e_row - fermi) / smearing))
        s_re, s_im = blochs[4]
        lhs = jnp.concatenate([s_re, s_im], axis=1)
        wides = [(b[0].astype(f32), b[1].astype(f32)) for b in blochs[1:4]]
        for a in range(3):
            v_re, v_im = blochs[1 + a]
            zero = jnp.zeros((32, 256), bf16)
            rhs = jnp.concatenate(
                [
                    jnp.concatenate([v_re, v_im], axis=1),
                    zero,
                    jnp.concatenate([-v_im, v_re], axis=1),
                    zero,
                ],
                axis=0,
            )
            prod = jnp.dot(lhs, rhs, preferred_element_type=f32)
            p_re = prod[:, 0:128]
            p_im = prod[:, 128:256]
            pad = jnp.zeros((32, 128), f32)
            t_re = flip(jnp.concatenate([p_re, pad], axis=0))[0:WF]
            t_im = flip(jnp.concatenate([p_im, pad], axis=0))[0:WF]
            c_re = (p_re + t_re) * 0.5 * weight
            c_im = (p_im - t_im) * 0.5 * weight
            for b in range(3):
                w_re, w_im = wides[b]
                curve = jnp.sum(c_re * w_im - c_im * w_re, axis=0, keepdims=True)
                keep_ref[3 * a + b, pl.ds(k, 1), :] = curve
                sum_ref[3 * a + b : 3 * a + b + 1, :] += occupation * curve

    @pl.when(step == pl.num_programs(0) - 1)
    def _():
        for ab in range(9):
            rows = jnp.concatenate([keep_ref[ab], jnp.zeros((112, 128), f32)], axis=0)
            curve_ref[ab] = flip(rows)[0:WF, 0:QUARTER]
        sums = sum_ref[0:8, :]
        last = jnp.broadcast_to(sum_ref[8:9, :], (8, 128))
        lane8 = lax.broadcasted_iota(jnp.int32, (8, 128), 1)
        row8 = lax.broadcasted_iota(jnp.int32, (8, 128), 0)
        extra = jnp.zeros((8, 128), f32)
        for t in range(3):
            extra = jnp.where(row8 == t, pltpu.roll(last, 96 - 32 * t, 1), extra)
        packed = jnp.where(lane8 < WF, sums, extra)
        total_ref[...] = packed


def bands(column, vectors, got, spin, fermi):
    per = QUARTER // PER_STEP
    grid_spec = pltpu.PrefetchScalarGridSpec(
        num_scalar_prefetch=1,
        grid=(per,),
        in_specs=[
            pl.BlockSpec((PER_STEP, 2, WF, WF), lambda i, c: (c[0] * per + i, 0, 0, 0)),
            pl.BlockSpec((GROUP, QUARTER, KEPT), lambda i, c: (0, 0, 0)),
            pl.BlockSpec((2, WF, WF), lambda i, c: (0, 0, 0)),
            pl.BlockSpec(memory_space=pltpu.SMEM),
        ],
        out_specs=[
            pl.BlockSpec((9, WF, QUARTER), lambda i, c: (0, 0, 0)),
            pl.BlockSpec((8, 128), lambda i, c: (0, 0)),
        ],
        scratch_shapes=[
            pltpu.VMEM((KEPT // 128, GROUP * QUARTER, 128), f32),
            pltpu.VMEM((PER_STEP, 256, 256), bf16),
            pltpu.VMEM((PER_STEP, 256, 256), bf16),
            pltpu.VMEM((WF, 256), bf16),
            pltpu.VMEM((PER_STEP, WF, 256), bf16),
            pltpu.VMEM((PER_STEP, 5, 256, 256), bf16),
            pltpu.VMEM((9, QUARTER, 128), f32),
            pltpu.VMEM((16, 128), f32),
        ],
    )

    def kernel(column_ref, *refs):
        bands_kernel(*refs)

    return pl.pallas_call(
        kernel,
        grid_spec=grid_spec,
        out_shape=[
            jax.ShapeDtypeStruct((9, WF, QUARTER), f32),
            jax.ShapeDtypeStruct((8, 128), f32),
        ],
        compiler_params=pltpu.CompilerParams(
            dimension_semantics=("arbitrary",), vmem_limit_bytes=40 << 20
        ),
        name="bands",
    )(column, vectors, got, spin, fermi)


def exchange(value, axes):
    return lax.all_to_all(value, axes, split_axis=0, concat_axis=0, tiled=True)


def on_device(hamiltonian, eigvecs, spin, k_indices, r_vectors, degeneracy, fermi_level):
    own = hamiltonian.shape[0]
    pieces = hamiltonian.reshape(own, 2, ROWS, GROUP, WF).transpose(3, 0, 2, 1, 4)
    pieces = pieces.reshape(GROUP, own, PIECE)
    points = jnp.zeros((own, WIDE - PIECE), bf16).at[0:3, :].set(k_indices.T.astype(bf16))
    points = jnp.broadcast_to(points[None], (GROUP, own, WIDE - PIECE))
    pieces = jnp.concatenate([pieces, points], axis=2)
    pieces = jnp.broadcast_to(pieces[None], (4, GROUP, own, WIDE)).reshape(4 * GROUP, own, WIDE)
    hopping = exchange(pieces, ALL)
    layer = lax.axis_index("z")
    mine = lax.dynamic_slice(hopping, (layer * GROUP, 0, 0), (GROUP, own, WIDE))
    k_rows = mine.reshape(8, 4, own, WIDE)[:, 0, :, PIECE:]
    k_rows = k_rows.transpose(0, 2, 1).reshape(8 * (WIDE - PIECE), own).astype(f32)
    lattice = jnp.concatenate(
        [r_vectors.T.astype(f32), jnp.broadcast_to(degeneracy.astype(f32)[None], (5, NR))], axis=0
    )
    entries = interpolate(k_rows, lattice, hopping.reshape(NR, WIDE))
    got = exchange(entries, PLANE)
    column = lax.axis_index("x").astype(jnp.int32).reshape(1)
    curvature, packed = bands(column, eigvecs, got, spin, fermi_level.reshape(1, 1))
    count = lax.axis_size("z") * lax.axis_size("y") * lax.axis_size("core") * lax.axis_size("x")
    copies = jnp.broadcast_to(packed[None], (count, 8, 128))
    total = jnp.sum(exchange(copies, ALL), axis=0) * (1.0 / math.sqrt(k_indices.shape[0] * 32))
    last = total[0:3, WF:].reshape(1, WF)
    totals = jnp.concatenate([total[:, :WF], last], axis=0)
    return (curvature, totals)


def solution(mesh):
    fine = Mesh(mesh.devices.reshape(4, 4, 2, 4), ALL)
    ka = ("z", "y", "core")
    in_specs = (P(ALL, None, None), P(ka, None, None, None), P(), P(ka, None), P(), P(), P())
    out_specs = (P(None, None, ALL), P())
    return jax.shard_map(
        on_device, mesh=fine, in_specs=in_specs, out_specs=out_specs, check_vma=False
    )
```

time: 236 us -> 122 us (0.52)
  local copies, waits for them, and re-layouts: 78.6 us -> 8.4 us
  matrix products: 41.4 us -> 0 us
  other arithmetic: 29.5 us -> 1.63 us
  Pallas kernels: 0 us -> 24.8 us
  waiting for transfers between devices: 40.1 us -> 64.3 us
  blocking collectives: 17.1 us -> 0 us
  between operations: 15.3 us -> 1.44 us
  starting transfers between devices: 12.4 us -> 21 us
    all_to_all x2 -> x3, waiting for transfers between devices: 19.1 us -> 64.3 us  [exchange(): return lax.all_to_all(value, axes, split_axis=0, concat_axis=0, tiled=True)]
    dot_general x23 -> x0, matrix products: 41.4 us -> none  [the longest x1 9.27 us: on_device(): summed = jnp.dot(phases, segment, preferred_element_type=jnp.float32)]
    pallas_call x0 -> x2, Pallas kernels: none -> 24.8 us  [the longest x1 13.3 us: bands(): pl.pallas_call(kernel, grid_spec=grid_spec, out_shape=[jax.ShapeDtypeStru...]
    all_gather x1 -> x0, waiting for transfers between devices: 20.9 us -> none  [on_device(): segment = lax.all_gather(entry_slice, 'ka', axis=0, tiled=True)]
    gather x4 -> x0, local copies, waits for them, and re-layouts: 20.2 us -> none  [the longest x1 8.64 us: phase_rows(): lattice_rows = jnp.take(lattice, vector_index, axis=0)]
    all_to_all x2 -> x0, blocking collectives: 17.1 us -> none  [the longest x1 10.6 us: on_device(): lax.all_to_all(flat_shard, 'col', split_axis=1, concat_axis=0, tiled=True)]
    another operation x5 -> x0, other arithmetic: 11.4 us -> none  [the longest x1 5.32 us: rotate(): return jnp.stack([sym_re, sym_im], axis=2).astype(jnp.bfloat16)]
    mul x3 -> x1, other arithmetic: 9.15 us -> 0.01 us  [on_device(): jnp.sum(exchange(copies, ALL), axis=0)]
  transfers between devices with their start and end apart: 3 -> 3, of which waited for: 3 -> 3; matrix products, arithmetic and copies ran while one was open for 22% -> 1% of each run, Pallas kernels for 0% -> 0%
where the time goes in v1:
time: 122 us
  waiting for transfers between devices  64.3 us (53%)
  Pallas kernels  24.8 us (20%)
  starting transfers between devices  21 us (17%)
  local copies, waits for them, and re-layouts  8.4 us (7%)
  other arithmetic  1.63 us (1%)
  between operations  1.44 us (1%)
    all_to_all x3, waiting for transfers between devices, exchange(): return lax.all_to_all(value, axes, split_axis=0, concat_axis=0, tiled=True)  64.3 us
    all_to_all x3, starting transfers between devices, exchange(): return lax.all_to_all(value, axes, split_axis=0, concat_axis=0, tiled=True)  21 us
    pallas_call x1, Pallas kernels, bands(): pl.pallas_call(kernel, grid_spec=grid_spec, out_shape=[jax.ShapeDtypeStru...  13.3 us
    pallas_call x1, Pallas kernels, interpolate(): pl.pallas_call(interpolate_kernel, grid=(GROUP * QUARTER // STEP_K,), in_...  11.5 us
    unnamed x11, local copies, waits for them, and re-layouts  4.11 us
  transfers between devices with their start and end apart: 3, of which 3 were waited for; matrix products, arithmetic and copies ran while one was open for 1% of the time, Pallas kernels for 0%

profile of v1, /device:TPU:1, one launch (start us, length us, event | category | flops | bytes accessed | tf_op | source)
XLA Modules:
  0.0 121.6 jit_solution(13200133011197373745)
XLA Ops:
  0.6 1.3 %reshape.69 = bf16[8,2,3,32,96]{4,3,2,1,0:T(8,128)(2,1)S(1)} reshape(bf16[8,2,9216]{2,1,0:T(2,128)(2,1)} %param.9) | data formatting | bytes 589824 | tf_op jit(solution)/shard_map/reshape | solution.py:322
  1.9 0.3 copy.17
  2.3 0.3 reshape.70
  2.6 0.7 convert_bitcast_fusion.2
  3.3 0.0 copy-start.4
  3.3 0.0 copy-start.3
  3.3 0.1 pad_maximum_fusion
  3.4 1.2 broadcast_in_dim.9
  4.6 11.5 %all-to-all-start = ((bf16[128,8,640]{2,1,0:T(8,128)(2,1)}), bf16[128,8,640]{2,1,0:T(8,128)(2,1)S(1)}, u32[]{:S(2)}, u32[]{:S(2)}) async-start(bf16[128,8,640]{2,1,0:T(8,128)(2,1)} %bitcast.3), calls=%async_computation | async-start | bytes 2621440 | tf_op jit(solution)/shard_map/all_to_all | solution.py:317
  16.1 0.0 copy-done.4
  16.1 0.0 copy-done.3
  16.2 22.3 %all-to-all-done = bf16[128,8,640]{2,1,0:T(8,128)(2,1)S(1)} async-done(((bf16[128,8,640]{2,1,0:T(8,128)(2,1)}), bf16[128,8,640]{2,1,0:T(8,128)(2,1)S(1)}, u32[]{:S(2)}, u32[]{:S(2)}) %all-to-all-start) | async-done | bytes 1310752 | tf_op jit(solution)/shard_map/all_to_all | solution.py:317
  38.5 0.1 convert_bitcast_fusion
  38.5 0.1 copy.14
  38.7 11.5 %interpolate.1 = bf16[32,16,2304]{2,1,0:T(8,128)(2,1)S(1)} custom-call(f32[512,8]{1,0:T(8,128)S(1)} %bitcast.23, f32[8,1024]{1,0:T(8,128)S(1)} %pad_maximum_fusion.1.lat_ref, bf16[1024,640]{1,0:T(8,128)(2,1)S(1)} %bitcast.22), custom_call_target="tpu_custom_call" | custom-call | tf_op jit(solution)/shard_map/interpolate/pallas_call | solution.py:107
  50.2 0.0 copy-start
  50.2 1.4 %copy-done = bf16[32,16,2304]{2,1,0:T(8,128)(2,1)} copy-done((bf16[32,16,2304]{2,1,0:T(8,128)(2,1)}, bf16[32,16,2304]{2,1,0:T(8,128)(2,1)S(1)}, u32[]{:S(2)}) %copy-start) | copy-done | bytes 2359320
  51.6 0.0 copy-start.2
  51.6 4.2 %all-to-all-start.1 = ((bf16[32,16,2304]{2,1,0:T(8,128)(2,1)}), bf16[32,16,2304]{2,1,0:T(8,128)(2,1)S(1)}, u32[]{:S(2)}, u32[]{:S(2)}) async-start(bf16[32,16,2304]{2,1,0:T(8,128)(2,1)} %copy-done), calls=%async_computation.1 | async-start | bytes 4718592 | tf_op jit(solution)/shard_map/all_to_all | solution.py:317
  56.4 29.0 %all-to-all-done.1.refs_1_ = bf16[32,16,2304]{2,1,0:T(8,128)(2,1)S(1)} async-done(((bf16[32,16,2304]{2,1,0:T(8,128)(2,1)}), bf16[32,16,2304]{2,1,0:T(8,128)(2,1)S(1)}, u32[]{:S(2)}, u32[]{:S(2)}) %all-to-all-start.1) | async-done | bytes 2359328 | tf_op jit(solution)/shard_map/all_to_all | solution.py:317
  85.4 0.0 copy-done.2
  85.4 0.0 copy-start.1
  85.4 1.9 %copy-done.1 = bf16[64,2,96,96]{3,2,1,0:T(8,128)(2,1)S(1)} copy-done((bf16[64,2,96,96]{3,2,1,0:T(8,128)(2,1)S(1)}, bf16[64,2,96,96]{3,2,1,0:T(8,128)(2,1)}, u32[]{:S(2)}) %copy-start.1) | copy-done | bytes 2359320
  87.3 13.3 %bands.1 = (f32[9,96,16]{2,1,0:T(8,128)S(1)}, f32[8,128]{1,0:T(8,128)S(1)}) custom-call(s32[1]{0:T(128)} %bitcast.column_ref, bf16[64,2,96,96]{3,2,1,0:T(8,128)(2,1)S(1)} %copy-done.1, bf16[32,16,2304]{2,1,0:T(8,128)(2,1)S(1)} %all-to-all-done.1.refs_1_, bf16[2,96,96]{2,1,0:T(8,128)(2,1)S(1)} %copy-done.2, f32[1,1]{1,0:T(1,128)} %bitcast.21.refs_3_), custom_call_target="tpu_custom_call" | custom-call | tf_op jit(solution)/shard_map/bands/pallas_call | solution.py:302
  100.6 0.8 broadcast_in_dim.11
  101.4 5.3 %all-to-all-start.2 = ((f32[128,8,128]{2,1,0:T(8,128)}), f32[128,8,128]{2,1,0:T(8,128)S(1)}, u32[]{:S(2)}, u32[]{:S(2)}) async-start(f32[128,8,128]{2,1,0:T(8,128)} %broadcast_in_dim.11), calls=%async_computation.2 | async-start | bytes 1048576 | tf_op jit(solution)/shard_map/all_to_all | solution.py:317
  106.7 0.8 copy.15
  107.5 13.1 %all-to-all-done.2 = f32[128,8,128]{2,1,0:T(8,128)S(1)} async-done(((f32[128,8,128]{2,1,0:T(8,128)}), f32[128,8,128]{2,1,0:T(8,128)S(1)}, u32[]{:S(2)}, u32[]{:S(2)}) %all-to-all-start.2) | async-done | bytes 524320 | tf_op jit(solution)/shard_map/all_to_all | solution.py:317
  120.6 0.1 reduce_sum.9
  120.8 0.1 slice.27
  120.9 0.1 reshape.75
  120.9 0.6 pad_maximum_fusion.2
  (8 shorter events, 0.1 us)
Async XLA Ops:
  3.3 12.8 %copy-start.4 = (s32[1024]{0:T(1024)S(1)}, s32[1024]{0:T(1024)}, u32[]{:S(2)}) copy-start(s32[1024]{0:T(1024)} %param.14) | copy-start | bytes 12292
  3.3 12.8 %copy-start.3 = (s32[1024,3]{0,1:T(4,128)S(1)}, s32[1024,3]{0,1:T(4,128)}, u32[]{:S(2)}) copy-start(s32[1024,3]{0,1:T(4,128)} %param.13) | copy-start | bytes 36868
  4.6 33.8 %all-to-all-start = ((bf16[128,8,640]{2,1,0:T(8,128)(2,1)}), bf16[128,8,640]{2,1,0:T(8,128)(2,1)S(1)}, u32[]{:S(2)}, u32[]{:S(2)}) async-start(bf16[128,8,640]{2,1,0:T(8,128)(2,1)} %bitcast.3), calls=%async_computation | async-start | bytes 2621440 | tf_op jit(solution)/shard_map/all_to_all | solution.py:317
  50.2 1.4 %copy-start = (bf16[32,16,2304]{2,1,0:T(8,128)(2,1)}, bf16[32,16,2304]{2,1,0:T(8,128)(2,1)S(1)}, u32[]{:S(2)}) copy-start(bf16[32,16,2304]{2,1,0:T(8,128)(2,1)S(1)} %interpolate.1) | copy-start | bytes 7077892
  51.6 33.8 %copy-start.2 = (bf16[2,96,96]{2,1,0:T(8,128)(2,1)S(1)}, bf16[2,96,96]{2,1,0:T(8,128)(2,1)}, u32[]{:S(2)}) copy-start(bf16[2,96,96]{2,1,0:T(8,128)(2,1)} %refs_2_.1) | copy-start | bytes 110596
  51.6 33.8 %all-to-all-start.1 = ((bf16[32,16,2304]{2,1,0:T(8,128)(2,1)}), bf16[32,16,2304]{2,1,0:T(8,128)(2,1)S(1)}, u32[]{:S(2)}, u32[]{:S(2)}) async-start(bf16[32,16,2304]{2,1,0:T(8,128)(2,1)} %copy-done), calls=%async_computation.1 | async-start | bytes 4718592 | tf_op jit(solution)/shard_map/all_to_all | solution.py:317
  85.4 1.9 %copy-start.1 = (bf16[64,2,96,96]{3,2,1,0:T(8,128)(2,1)S(1)}, bf16[64,2,96,96]{3,2,1,0:T(8,128)(2,1)}, u32[]{:S(2)}) copy-start(bf16[64,2,96,96]{3,2,1,0:T(8,128)(2,1)} %refs_0_.1) | copy-start | bytes 7077892
  101.4 19.2 %all-to-all-start.2 = ((f32[128,8,128]{2,1,0:T(8,128)}), f32[128,8,128]{2,1,0:T(8,128)S(1)}, u32[]{:S(2)}, u32[]{:S(2)}) async-start(f32[128,8,128]{2,1,0:T(8,128)} %broadcast_in_dim.11), calls=%async_computation.2 | async-start | bytes 1048576 | tf_op jit(solution)/shard_map/all_to_all | solution.py:317

commit v2 on v0

v2 whole, which is shorter than its diff:
```python
import math

import jax
import jax.numpy as jnp
from jax import lax
from jax.experimental import pallas as pl
from jax.experimental.pallas import tpu as pltpu
from jax.sharding import Mesh, PartitionSpec as P

WF = 96
GRID = 64
NR = 1024
GROUP = 32
ROWS = 3
PIECE = ROWS * 2 * WF
WIDE = 640
KEPT = 4 * PIECE
QUARTER = 16
PITCH = 17
STEP_K = 128
PER_STEP = 4
SIDE_STEP = 4

broadening = 0.5
smearing = 0.1

ALL = ("z", "y", "core", "x")
PLANE = ("y", "core", "x")

f32 = jnp.float32
bf16 = jnp.bfloat16

SINE = (3.14159264, -5.16771009, 2.55007766, -0.59829216, 0.07765941)
COSINE = (0.99999995, -4.93479286, 4.05841192, -1.33188016, 0.2196968)


def whole(shape):
    return pl.BlockSpec(shape, lambda *_: (0,) * len(shape))


def horner(coefficients, q):
    value = coefficients[-1]
    for c in coefficients[-2::-1]:
        value = value * q + c
    return value


def turn(f):
    q = f * f
    s = f * horner(SINE, q)
    twice = s + s
    return 1.0 - twice * s, twice * horner(COSINE, q)


def flip(x):
    return jnp.transpose(x, (1, 0))


def flip_square(x):
    pad = jnp.zeros((32, 128), f32)
    return flip(jnp.concatenate([x, pad], axis=0))[0:WF]


def turn_hopping(hop_ref, w_ref):
    lane = lax.broadcasted_iota(jnp.int32, (NR, 128), 1)
    tiles = [hop_ref[:, 128 * t : 128 * (t + 1)].astype(f32) for t in range(5)]
    tiles[4] = jnp.where(lane < 64, tiles[4], 0.0)
    ups = [pltpu.roll(t, 96, 1) for t in tiles]
    downs = [pltpu.roll(t, 32, 1) for t in tiles]
    for t in range(5):
        w_ref[0:NR, 128 * t : 128 * (t + 1)] = tiles[t].astype(bf16)
        up = jnp.where(lane < 96, ups[(t - 1) % 5], ups[t])
        down = jnp.where(lane < 32, downs[t], downs[(t + 1) % 5])
        place = (lane + 128 * t) % (2 * WF)
        turned = jnp.where(place < WF, -down, up)
        if t == 4:
            turned = jnp.where(lane < 64, turned, 0.0)
        w_ref[NR : 2 * NR, 128 * t : 128 * (t + 1)] = turned.astype(bf16)


def phase_block(k, lat_ref, p_ref):
    r = [lat_ref[a : a + 1, :] for a in range(3)]
    inverse = 1.0 / lat_ref[3:4, :]
    turns = sum(k[:, a : a + 1] * (r[a] * (1.0 / GRID)) for a in range(3))
    cosine, sine = turn(turns - jnp.floor(turns + 0.5))
    for c in range(4):
        rows = slice(c * STEP_K, (c + 1) * STEP_K)
        if c == 0:
            re, im = cosine * inverse, sine * inverse
        else:
            coord = r[c - 1] * inverse
            re, im = sine * (-coord), cosine * coord
        p_ref[rows, 0:NR] = re.astype(bf16)
        p_ref[rows, NR : 2 * NR] = im.astype(bf16)


def interpolate_kernel(k_ref, lat_ref, hop_ref, out_ref, w_ref, *p_refs):
    steps = GROUP * QUARTER // STEP_K
    per = STEP_K // QUARTER
    lane = lax.broadcasted_iota(jnp.int32, (STEP_K, 128), 1)

    def phases(i):
        phase_block(k_ref[i * STEP_K : (i + 1) * STEP_K, :], lat_ref, p_refs[i % 2])

    phases(0)
    turn_hopping(hop_ref, w_ref)
    for i in range(steps):
        if i + 1 < steps:
            phases(i + 1)
        summed = jnp.dot(p_refs[i % 2][...], w_ref[...], preferred_element_type=f32)
        for pair in range(2):
            even = summed[2 * pair * STEP_K : (2 * pair + 1) * STEP_K]
            odd = summed[(2 * pair + 1) * STEP_K : (2 * pair + 2) * STEP_K]
            shifted = [pltpu.roll(odd[:, 128 * t : 128 * (t + 1)], 64, 1) for t in range(5)]
            for t in range(9):
                if t < 4:
                    tile = even[:, 128 * t : 128 * (t + 1)]
                elif t == 4:
                    tile = jnp.where(lane < 64, even[:, 512:640], shifted[0])
                else:
                    tile = jnp.where(lane < 64, shifted[t - 5], shifted[t - 4])
                at = pair * 2 * PIECE + 128 * t
                value = tile.reshape(per, QUARTER, 128).astype(bf16)
                out_ref[i * per : (i + 1) * per, :, at : at + 128] = value


def interpolate(k_rows, lattice, hopping):
    vmem = pl.BlockSpec(memory_space=pltpu.VMEM)
    return pl.pallas_call(
        interpolate_kernel,
        in_specs=[vmem, vmem, vmem],
        out_specs=vmem,
        out_shape=jax.ShapeDtypeStruct((GROUP, QUARTER, KEPT), bf16),
        scratch_shapes=[
            pltpu.VMEM((2 * NR, WIDE), bf16),
            pltpu.VMEM((4 * STEP_K, 2 * NR), bf16),
            pltpu.VMEM((4 * STEP_K, 2 * NR), bf16),
        ],
        compiler_params=pltpu.CompilerParams(vmem_limit_bytes=30 << 20),
        name="interpolate",
    )(k_rows, lattice, hopping)


def rotate(ut, half):
    h_re, h_im = half[:, 0:128], half[:, 128:256]
    zero = jnp.zeros((32, 256), bf16)
    rhs = jnp.concatenate(
        [half, zero, jnp.concatenate([h_im, -h_re], axis=1), zero], axis=0
    )
    full = jnp.dot(ut, rhs, preferred_element_type=f32)
    return full[:, 0:128], full[:, 128:256]


def hermitian(re, im):
    return (re + flip_square(re)) * 0.5, (im - flip_square(im)) * 0.5


def sides_kernel(column_ref, vec_ref, spin_ref, fermi_ref, wu_ref, ut_ref, sb_ref, level_ref, sp_ref):
    @pl.when(pl.program_id(0) == 0)
    def _():
        level_ref[...] = jnp.full(level_ref.shape, fermi_ref[0, 0], f32)
        sp_ref[...] = jnp.zeros_like(sp_ref)
        spin_re = spin_ref[0].astype(f32)
        spin_im = spin_ref[1].astype(f32)
        sp_ref[:, 0:WF] = ((spin_re + flip(spin_re)) * 0.5).astype(bf16)
        sp_ref[:, WF : 2 * WF] = ((spin_im - flip(spin_im)) * 0.5).astype(bf16)

    wu_ref[...] = jnp.zeros_like(wu_ref)
    ut_ref[...] = jnp.zeros_like(ut_ref)
    for q in range(SIDE_STEP):
        u_re = vec_ref[q, 0]
        u_im = vec_ref[q, 1]
        wu_ref[q, 64 : 64 + WF, 0:WF] = u_re
        wu_ref[q, 64 : 64 + WF, 128 : 128 + WF] = u_im
        wu_ref[q, 160 : 160 + WF, 0:WF] = -u_im
        wu_ref[q, 160 : 160 + WF, 128 : 128 + WF] = u_re
        ut_ref[q, :, 0:WF] = flip(u_re.astype(f32)).astype(bf16)
        ut_ref[q, :, 128 : 128 + WF] = flip(u_im.astype(f32)).astype(bf16)
    for q in range(SIDE_STEP):
        half = jnp.dot(sp_ref[...], wu_ref[q, 64:320, :], preferred_element_type=f32)
        s_re, s_im = hermitian(*rotate(ut_ref[q], half.astype(bf16)))
        sb_ref[q, :, 0:128] = s_re.astype(bf16)
        sb_ref[q, :, 128:256] = s_im.astype(bf16)


def sides(column, vectors, spin, fermi):
    per = QUARTER // SIDE_STEP
    shapes = [(320, 256), (WF, 256), (WF, 256)]
    grid_spec = pltpu.PrefetchScalarGridSpec(
        num_scalar_prefetch=1,
        grid=(per,),
        in_specs=[
            pl.BlockSpec((SIDE_STEP, 2, WF, WF), lambda i, c: (c[0] * per + i, 0, 0, 0)),
            whole((2, WF, WF)),
            pl.BlockSpec(memory_space=pltpu.SMEM),
        ],
        out_specs=[pl.BlockSpec((SIDE_STEP, *s), lambda i, c: (i, 0, 0)) for s in shapes]
        + [whole((8, 128))],
        scratch_shapes=[pltpu.VMEM((WF, 256), bf16)],
    )
    return pl.pallas_call(
        sides_kernel,
        grid_spec=grid_spec,
        out_shape=[jax.ShapeDtypeStruct((QUARTER, *s), bf16) for s in shapes]
        + [jax.ShapeDtypeStruct((8, 128), f32)],
        compiler_params=pltpu.CompilerParams(
            dimension_semantics=("arbitrary",), vmem_limit_bytes=30 << 20
        ),
        cost_estimate=pl.CostEstimate(
            flops=QUARTER * 4 * 256 * 256 * 256,
            transcendentals=0,
            bytes_accessed=QUARTER * 2 * 256 * (320 + 4 * WF),
        ),
        name="sides",
    )(column, vectors, spin, fermi)


def bands_kernel(
    wu_ref, ut_ref, sb_ref, got_ref, level_ref, curve_ref, total_ref,
    wide_ref, half_ref, bloch_ref, sum_ref,
):
    step = pl.program_id(0)

    @pl.when(step == 0)
    def _():
        for t in range(KEPT // 128):
            tile = got_ref[:, :, 128 * t : 128 * (t + 1)].astype(f32)
            for s in range(GROUP):
                wide_ref[t, PITCH * s : PITCH * s + QUARTER, :] = tile[s]
        sum_ref[...] = jnp.zeros_like(sum_ref)

    lane = lax.broadcasted_iota(jnp.int32, (WF, 128), 1)
    row = lax.broadcasted_iota(jnp.int32, (WF, 128), 0)
    eye = lane == row
    fermi = level_ref[0:1, :]
    zero = jnp.zeros((32, 256), bf16)
    mine = range(PER_STEP)

    where = {}
    for c in range(4):
        for r in range(ROWS):
            at = c * PIECE + r * 2 * WF
            odd = at % 128 != 0
            where[c, r] = (odd, 32 * sum(1 for w in where.values() if w[0] == odd), at // 128)
    for q in mine:
        k = step * PER_STEP + q
        for odd, at in ((False, 64), (True, 0)):
            rows = jnp.concatenate(
                [
                    jnp.concatenate(
                        [
                            wide_ref[w[2] + j, pl.ds(k, GROUP, stride=PITCH), :].astype(bf16)
                            for j in range(2)
                        ],
                        axis=1,
                    )
                    for w in where.values()
                    if w[0] == odd
                ],
                axis=0,
            )
            weights = wu_ref[q, at : at + 256, :]
            half = jnp.dot(rows, weights, preferred_element_type=f32).astype(bf16)
            for (c, r), w in where.items():
                if w[0] == odd:
                    half_ref[q, c, 32 * r : 32 * r + 32, :] = half[w[1] : w[1] + 32]
    for q in mine:
        for c in range(4):
            b_re, b_im = hermitian(*rotate(ut_ref[q], half_ref[q, c]))
            bloch_ref[q, c, :, 0:128] = b_re.astype(bf16)
            bloch_ref[q, c, :, 128:256] = b_im.astype(bf16)
    for q in mine:
        k = step * PER_STEP + q
        diag = jnp.where(eye, bloch_ref[q, 0, :, 0:128].astype(f32), 0.0)
        e_row = jnp.sum(diag, axis=0, keepdims=True)
        e_col = jnp.sum(diag, axis=1, keepdims=True)
        gap = e_col - e_row
        weight = -1.0 / (gap * gap + broadening * broadening)
        occupation = 1.0 / (1.0 + jnp.exp((e_row - fermi) / smearing))
        for a in range(3):
            v = bloch_ref[q, 1 + a]
            v_re, v_im = v[:, 0:128], v[:, 128:256]
            rhs = jnp.concatenate(
                [v, zero, jnp.concatenate([-v_im, v_re], axis=1), zero], axis=0
            )
            prod = jnp.dot(sb_ref[q], rhs, preferred_element_type=f32)
            p_re = prod[:, 0:128]
            p_im = prod[:, 128:256]
            c_re = (p_re + flip_square(p_re)) * weight
            c_im = (p_im - flip_square(p_im)) * weight
            for b in range(3):
                w_re = bloch_ref[q, 1 + b, :, 0:128].astype(f32)
                w_im = bloch_ref[q, 1 + b, :, 128:256].astype(f32)
                curve = jnp.sum(c_re * w_im - c_im * w_re, axis=0, keepdims=True)
                curve_ref[3 * a + b, pl.ds(k, 1), :] = curve[:, 0:WF]
                sum_ref[3 * a + b : 3 * a + b + 1, :] += occupation * curve

    @pl.when(step == pl.num_programs(0) - 1)
    def _():
        last = jnp.broadcast_to(sum_ref[8:9, :], (8, 128))
        lane8 = lax.broadcasted_iota(jnp.int32, (8, 128), 1)
        row8 = lax.broadcasted_iota(jnp.int32, (8, 128), 0)
        extra = jnp.zeros((8, 128), f32)
        for t in range(3):
            extra = jnp.where(row8 == t, pltpu.roll(last, 96 - 32 * t, 1), extra)
        packed = jnp.where(lane8 < WF, sum_ref[0:8, :], extra)
        total_ref[...] = jnp.broadcast_to(packed[None], total_ref.shape)


def bands(count, prepared, got, level):
    per = QUARTER // PER_STEP
    shapes = [(9, QUARTER, WF), (count, 8, 128)]
    return pl.pallas_call(
        bands_kernel,
        grid=(per,),
        in_specs=[
            pl.BlockSpec((PER_STEP, *p.shape[1:]), lambda i: (i, 0, 0)) for p in prepared
        ]
        + [pl.BlockSpec(memory_space=pltpu.VMEM)] * 2,
        out_specs=[pl.BlockSpec(memory_space=pltpu.VMEM) for _ in shapes],
        out_shape=[jax.ShapeDtypeStruct(shape, f32) for shape in shapes],
        scratch_shapes=[
            pltpu.VMEM((KEPT // 128, GROUP * PITCH, 128), f32),
            pltpu.VMEM((PER_STEP, 4, WF, 256), bf16),
            pltpu.VMEM((PER_STEP, 4, WF, 256), bf16),
            pltpu.VMEM((16, 128), f32),
        ],
        compiler_params=pltpu.CompilerParams(
            dimension_semantics=("arbitrary",), vmem_limit_bytes=30 << 20
        ),
        name="bands",
    )(*prepared, got, level)


def exchange(value, axes):
    return lax.all_to_all(value, axes, split_axis=0, concat_axis=0, tiled=True)


def on_device(hamiltonian, eigvecs, spin, k_indices, r_vectors, degeneracy, fermi_level):
    own = hamiltonian.shape[0]
    pieces = hamiltonian.reshape(own, 2, ROWS, GROUP, WF).transpose(3, 0, 2, 1, 4)
    pieces = pieces.reshape(GROUP, own, PIECE)
    points = jnp.zeros((own, WIDE - PIECE), bf16).at[0:3, :].set(k_indices.T.astype(bf16))
    points = jnp.broadcast_to(points[None], (GROUP, own, WIDE - PIECE))
    pieces = jnp.concatenate([pieces, points], axis=2)
    pieces = jnp.broadcast_to(pieces[None], (4, GROUP, own, WIDE)).reshape(4 * GROUP, own, WIDE)
    hopping = exchange(pieces, ALL)
    column = lax.axis_index("x").astype(jnp.int32).reshape(1)
    vectors = pltpu.with_memory_space_constraint(eigvecs, pltpu.HBM)
    *prepared, level = sides(column, vectors, spin, fermi_level.reshape(1, 1))
    prepared = [pltpu.with_memory_space_constraint(p, pltpu.HBM) for p in prepared]
    layer = lax.axis_index("z")
    mine = lax.dynamic_slice(hopping, (layer * GROUP, 0, 0), (GROUP, own, WIDE))
    k_rows = mine.reshape(8, 4, own, WIDE)[:, 0, :, PIECE:]
    k_rows = k_rows.transpose(0, 2, 1).reshape(8 * (WIDE - PIECE), own).astype(f32)
    lattice = jnp.concatenate(
        [r_vectors.T.astype(f32), jnp.broadcast_to(degeneracy.astype(f32)[None], (5, NR))], axis=0
    )
    entries = interpolate(k_rows, lattice, hopping.reshape(NR, WIDE))
    entries, level, *prepared = lax.optimization_barrier((entries, level, *prepared))
    got = exchange(entries, PLANE)
    count = lax.axis_size("z") * lax.axis_size("y") * lax.axis_size("core") * lax.axis_size("x")
    curvature, copies = bands(count, prepared, got, level)
    total_points = k_indices.shape[0] * count // 4
    total = jnp.sum(exchange(copies, ALL), axis=0) * (1.0 / math.sqrt(total_points))
    last = total[0:3, WF:].reshape(1, WF)
    totals = jnp.concatenate([total[:, :WF], last], axis=0)
    return (curvature.transpose(0, 2, 1), totals)


def solution(mesh):
    fine = Mesh(mesh.devices.reshape(4, 4, 2, 4), ALL)
    ka = ("z", "y", "core")
    in_specs = (P(ALL, None, None), P(ka, None, None, None), P(), P(ka, None), P(), P(), P())
    out_specs = (P(None, None, ALL), P())
    return jax.shard_map(
        on_device, mesh=fine, in_specs=in_specs, out_specs=out_specs, check_vma=False
    )
```

time: 236 us -> 111 us (0.47)
  local copies, waits for them, and re-layouts: 78.6 us -> 6.75 us
  matrix products: 41.4 us -> 0 us
  blocking collectives: 17.1 us -> 52.6 us
  other arithmetic: 29.5 us -> 1.63 us
  waiting for transfers between devices: 40.1 us -> 12.9 us
  Pallas kernels: 0 us -> 23.7 us
  between operations: 15.3 us -> 1.44 us
    dot_general x23 -> x0, matrix products: 41.4 us -> none  [the longest x1 9.27 us: on_device(): summed = jnp.dot(phases, segment, preferred_element_type=jnp.float32)]
    all_to_all x2, blocking collectives: 17.1 us -> 52.6 us  [exchange(): return lax.all_to_all(value, axes, split_axis=0, concat_axis=0, tiled=True)]
    pallas_call x0 -> x3, Pallas kernels: none -> 23.7 us  [the longest x1 9.97 us: bands(): pl.pallas_call(bands_kernel, grid=(per,), in_specs=[pl.BlockSpec((PER_STE...]
    all_gather x1 -> x0, waiting for transfers between devices: 20.9 us -> none  [on_device(): segment = lax.all_gather(entry_slice, 'ka', axis=0, tiled=True)]
    gather x4 -> x0, local copies, waits for them, and re-layouts: 20.2 us -> none  [the longest x1 8.64 us: phase_rows(): lattice_rows = jnp.take(lattice, vector_index, axis=0)]
    another operation x5 -> x0, other arithmetic: 11.4 us -> none  [the longest x1 5.32 us: rotate(): return jnp.stack([sym_re, sym_im], axis=2).astype(jnp.bfloat16)]
    mul x3 -> x1, other arithmetic: 9.15 us -> 0.01 us  [on_device(): jnp.sum(exchange(copies, ALL), axis=0) * (1.0 / math.sqrt(total_points))]
    add x3 -> x0, local copies, waits for them, and re-layouts: 8.01 us -> none  [the longest x2 6.04 us: rotate(): jnp.einsum('kjn,kcjm->kcnm', vec_re, half_re, preferred_element_type=jnp....]
  transfers between devices with their start and end apart: 3 -> 1, of which waited for: 3 -> 1; matrix products, arithmetic and copies ran while one was open for 22% -> 0% of each run, Pallas kernels for 0% -> 5%
where the time goes in v2:
time: 111 us
  blocking collectives  52.6 us (47%)
  Pallas kernels  23.7 us (21%)
  waiting for transfers between devices  12.9 us (12%)
  starting transfers between devices  11.5 us (10%)
  local copies, waits for them, and re-layouts  6.75 us (6%)
  other arithmetic  1.63 us (1%)
  between operations  1.44 us (1%)
    all_to_all x2, blocking collectives, exchange(): return lax.all_to_all(value, axes, split_axis=0, concat_axis=0, tiled=True)  52.6 us
    all_to_all x1, waiting for transfers between devices, exchange(): return lax.all_to_all(value, axes, split_axis=0, concat_axis=0, tiled=True)  12.9 us
    all_to_all x1, starting transfers between devices, exchange(): return lax.all_to_all(value, axes, split_axis=0, concat_axis=0, tiled=True)  11.5 us
    pallas_call x1, Pallas kernels, bands(): pl.pallas_call(bands_kernel, grid=(per,), in_specs=[pl.BlockSpec((PER_STE...  9.97 us
    pallas_call x1, Pallas kernels, interpolate(): pl.pallas_call(interpolate_kernel, in_specs=[vmem, vmem, vmem], out_specs...  8.34 us
    pallas_call x1, Pallas kernels, sides(): pl.pallas_call(sides_kernel, grid_spec=grid_spec, out_shape=[jax.ShapeDty...  5.38 us
    unnamed x12, local copies, waits for them, and re-layouts  3.33 us
  transfers between devices with their start and end apart: 1, of which 1 were waited for; matrix products, arithmetic and copies ran while one was open for 0% of the time, Pallas kernels for 5%

profile of v2, /device:TPU:1, one launch (start us, length us, event | category | flops | bytes accessed | tf_op | source)
XLA Modules:
  0.0 110.5 jit_solution(12373446051360379903)
XLA Ops:
  0.6 0.7 convert_bitcast_fusion.2
  1.3 1.3 %reshape.67 = bf16[8,2,3,32,96]{4,3,2,1,0:T(8,128)(2,1)S(1)} reshape(bf16[8,2,9216]{2,1,0:T(2,128)(2,1)} %param.9) | data formatting | bytes 589824 | tf_op jit(solution)/shard_map/reshape | solution.py:341
  2.6 0.3 copy.12
  2.9 0.3 reshape.68
  3.3 0.0 copy-start.5
  3.3 0.0 copy-start.3
  3.3 0.1 pad_maximum_fusion
  3.4 1.2 %broadcast_in_dim.7 = bf16[4,32,8,640]{3,2,1,0:T(8,128)(2,1)} broadcast(bf16[32,8,640]{2,1,0:T(8,128)(2,1)S(1)} %pad_maximum_fusion), dimensions={1,2,3} | broadcast | bytes 1638400 | tf_op jit(solution)/shard_map/broadcast_in_dim | solution.py:346
  4.6 11.5 %all-to-all-start = ((bf16[128,8,640]{2,1,0:T(8,128)(2,1)}), bf16[128,8,640]{2,1,0:T(8,128)(2,1)S(1)}, u32[]{:S(2)}, u32[]{:S(2)}) async-start(bf16[128,8,640]{2,1,0:T(8,128)(2,1)} %bitcast.2), calls=%async_computation | async-start | bytes 2621440 | tf_op jit(solution)/shard_map/all_to_all | solution.py:336
  16.1 0.0 copy-start.4
  16.7 0.0 copy-done.5
  16.8 0.0 copy-done.3
  16.8 5.4 %sides.1 = (bf16[16,320,256]{2,1,0:T(8,128)(2,1)S(1)}, bf16[16,96,256]{2,1,0:T(8,128)(2,1)S(1)}, bf16[16,96,256]{2,1,0:T(8,128)(2,1)S(1)}, f32[8,128]{1,0:T(8,128)S(1)}) custom-call(s32[1]{0:T(128)} %bitcast.9.column_ref, bf16[64,2,96,96]{3,2,1,0:T(8,128)(2,1)} %vec_ref.1, bf16[2,96,96]{2,1,0:T(8,128)(2,1)S(1)} %copy-done.3, f32[1,1]{1,0:T(1,128)} %bitcast.22.fermi_ref), custom_call_target="tpu_custom_call" | custom-call | flops 1073741824 | bytes 5767168 | tf_op jit(solution)/shard_map/sides/pallas_call | solution.py:201
  22.2 0.0 copy-start
  22.2 1.5 %copy-done = bf16[16,320,256]{2,1,0:T(8,128)(2,1)} copy-done((bf16[16,320,256]{2,1,0:T(8,128)(2,1)}, bf16[16,320,256]{2,1,0:T(8,128)(2,1)S(1)}, u32[]{:S(2)}) %copy-start) | copy-done | bytes 2621464
  23.7 0.0 copy-start.1
  23.7 0.9 copy-done.1
  24.6 0.0 copy-start.2
  24.6 0.9 copy-done.2
  25.5 0.0 copy-done.4
  25.5 12.9 %all-to-all-done = bf16[128,8,640]{2,1,0:T(8,128)(2,1)S(1)} async-done(((bf16[128,8,640]{2,1,0:T(8,128)(2,1)}), bf16[128,8,640]{2,1,0:T(8,128)(2,1)S(1)}, u32[]{:S(2)}, u32[]{:S(2)}) %all-to-all-start) | async-done | bytes 1310752 | tf_op jit(solution)/shard_map/all_to_all | solution.py:336
  38.4 0.1 convert_bitcast_fusion
  38.5 0.1 copy.10
  38.7 8.3 %interpolate.1 = bf16[32,16,2304]{2,1,0:T(8,128)(2,1)S(1)} custom-call(f32[512,8]{1,0:T(8,128)S(1)} %bitcast.24, f32[8,1024]{1,0:T(8,128)S(1)} %pad_maximum_fusion.1.lat_ref, bf16[1024,640]{1,0:T(8,128)(2,1)S(1)} %bitcast.23), custom_call_target="tpu_custom_call" | custom-call | tf_op jit(solution)/shard_map/interpolate/pallas_call | solution.py:129
  47.0 34.7 %all_to_all.15.got_ref = bf16[32,16,2304]{2,1,0:T(8,128)(2,1)S(1)} all-to-all(bf16[32,16,2304]{2,1,0:T(8,128)(2,1)S(1)} %interpolate.1), channel_id=1, replica_groups=mesh['z'=4,'y'=4,'core'=2,'x'=4] {'y','core','x'}, dimensions={0} | all-to-all | bytes 4718592 | tf_op jit(solution)/shard_map/all_to_all | solution.py:336
  81.7 10.0 %bands.1 = (f32[9,16,96]{2,1,0:T(8,128)}, f32[128,8,128]{2,1,0:T(8,128)S(1)}) custom-call(bf16[16,320,256]{2,1,0:T(8,128)(2,1)} %copy-done, bf16[16,96,256]{2,1,0:T(8,128)(2,1)} %copy-done.1, bf16[16,96,256]{2,1,0:T(8,128)(2,1)} %copy-done.2, bf16[32,16,2304]{2,1,0:T(8,128)(2,1)S(1)} %all_to_all.15.got_ref, f32[8,128]{1,0:T(8,128)S(1)} %get-tuple-element.33.level_ref), custom_call_target="tpu_custom_call" | custom-call | tf_op jit(solution)/shard_map/bands/pallas_call | solution.py:313
  91.6 18.0 %all_to_all.16 = f32[128,8,128]{2,1,0:T(8,128)S(1)} all-to-all(f32[128,8,128]{2,1,0:T(8,128)S(1)} %get-tuple-element.35), channel_id=1, replica_groups=mesh['z'=4,'y'=4,'core'=2,'x'=4] {'z','y','core','x'}, dimensions={0} | all-to-all | bytes 1048576 | tf_op jit(solution)/shard_map/all_to_all | solution.py:336
  109.6 0.1 reduce_sum.9
  109.7 0.1 slice.27
  109.8 0.1 reshape.74
  109.9 0.6 pad_maximum_fusion.2
  (8 shorter events, 0.1 us)
Async XLA Ops:
  3.3 13.4 %copy-start.5 = (s32[1024]{0:T(1024)S(1)}, s32[1024]{0:T(1024)}, u32[]{:S(2)}) copy-start(s32[1024]{0:T(1024)} %param.14) | copy-start | bytes 12292
  3.3 13.5 %copy-start.3 = (bf16[2,96,96]{2,1,0:T(8,128)(2,1)S(1)}, bf16[2,96,96]{2,1,0:T(8,128)(2,1)}, u32[]{:S(2)}) copy-start(bf16[2,96,96]{2,1,0:T(8,128)(2,1)} %spin_ref.1) | copy-start | bytes 110596
  4.6 33.8 %all-to-all-start = ((bf16[128,8,640]{2,1,0:T(8,128)(2,1)}), bf16[128,8,640]{2,1,0:T(8,128)(2,1)S(1)}, u32[]{:S(2)}, u32[]{:S(2)}) async-start(bf16[128,8,640]{2,1,0:T(8,128)(2,1)} %bitcast.2), calls=%async_computation | async-start | bytes 2621440 | tf_op jit(solution)/shard_map/all_to_all | solution.py:336
  16.1 9.4 %copy-start.4 = (s32[1024,3]{0,1:T(4,128)S(1)}, s32[1024,3]{0,1:T(4,128)}, u32[]{:S(2)}) copy-start(s32[1024,3]{0,1:T(4,128)} %param.13) | copy-start | bytes 36868
  22.2 1.5 %copy-start = (bf16[16,320,256]{2,1,0:T(8,128)(2,1)}, bf16[16,320,256]{2,1,0:T(8,128)(2,1)S(1)}, u32[]{:S(2)}) copy-start(bf16[16,320,256]{2,1,0:T(8,128)(2,1)S(1)} %get-tuple-element.29.wu_ref) | copy-start | bytes 7864324
  23.7 0.9 copy-start.1
  24.6 0.9 copy-start.2

commit v3 on v2

--- a/solution.py
+++ b/solution.py
@@ -59,6 +59,73 @@
 def flip_square(x):
     pad = jnp.zeros((32, 128), f32)
     return flip(jnp.concatenate([x, pad], axis=0))[0:WF]
+
+
+def pack_kernel(ham_ref, k_ref, out_ref, piece_ref, points_ref, sems):
+    lane = lax.broadcasted_iota(jnp.int32, (8, 128), 1)
+    points_ref[...] = jnp.zeros_like(points_ref)
+    points_ref[0:3, 64:128] = k_ref[...].astype(f32)
+    points = points_ref[...]
+    loaded = {}
+
+    def tile(part, t):
+        if (part, t) not in loaded:
+            loaded[part, t] = ham_ref[:, part, 128 * t : 128 * (t + 1)].astype(f32)
+        return loaded[part, t]
+
+    def segment(part, line, start, size, at):
+        first = WF * line + start
+        shift = (at - first) % 128
+        move = lambda t: pltpu.roll(tile(part, t), shift, 1) if shift else tile(part, t)
+        value = move(first // 128)
+        if (first + size - 1) // 128 != first // 128:
+            cut = at + 128 - first % 128
+            value = jnp.where(lane < cut, value, move(first // 128 + 1))
+        return value
+
+    layout = [
+        ((0, 0, 0, 96, 0), (1, 0, 0, 32, 96)),
+        ((1, 0, 32, 64, 0), (0, 1, 0, 64, 64)),
+        ((0, 1, 64, 32, 0), (1, 1, 0, 96, 32)),
+        ((0, 2, 0, 96, 0), (1, 2, 0, 32, 96)),
+        ((1, 2, 32, 64, 0), None),
+    ]
+    for g in range(GROUP):
+        for t, (left, right) in enumerate(layout):
+            part, r, start, size, at = left
+            value = segment(part, GROUP * r + g, start, size, at)
+            if right is None:
+                other = points
+            else:
+                other = segment(right[0], GROUP * right[1] + g, *right[2:])
+            value = jnp.where(lane < size, value, other)
+            piece_ref[g, :, 128 * t : 128 * (t + 1)] = value.astype(bf16)
+    layers = out_ref.shape[0] // GROUP
+    copies = [
+        pltpu.make_async_copy(piece_ref, out_ref.at[pl.ds(GROUP * z, GROUP)], sems.at[z])
+        for z in range(layers)
+    ]
+    for copy in copies:
+        copy.start()
+    for copy in copies:
+        copy.wait()
+
+
+def pack(hamiltonian, k_rows, count):
+    own = hamiltonian.shape[0]
+    vmem = pl.BlockSpec(memory_space=pltpu.VMEM)
+    return pl.pallas_call(
+        pack_kernel,
+        in_specs=[vmem, vmem],
+        out_specs=pl.BlockSpec(memory_space=pl.ANY),
+        out_shape=jax.ShapeDtypeStruct((count, own, WIDE), bf16),
+        scratch_shapes=[
+            pltpu.VMEM((GROUP, own, WIDE), bf16),
+            pltpu.VMEM((8, 128), f32),
+            pltpu.SemaphoreType.DMA((count // GROUP,)),
+        ],
+        name="pack",
+    )(hamiltonian, k_rows)
 
 
 def turn_hopping(hop_ref, w_ref):
@@ -217,24 +284,18 @@
 
 def bands_kernel(
     wu_ref, ut_ref, sb_ref, got_ref, level_ref, curve_ref, total_ref,
-    wide_ref, half_ref, bloch_ref, sum_ref,
+    wide_ref, half_ref, *bloch_refs,
 ):
-    step = pl.program_id(0)
-
-    @pl.when(step == 0)
-    def _():
-        for t in range(KEPT // 128):
-            tile = got_ref[:, :, 128 * t : 128 * (t + 1)].astype(f32)
-            for s in range(GROUP):
-                wide_ref[t, PITCH * s : PITCH * s + QUARTER, :] = tile[s]
-        sum_ref[...] = jnp.zeros_like(sum_ref)
+    for t in range(KEPT // 128):
+        tile = got_ref[:, :, 128 * t : 128 * (t + 1)].astype(f32)
+        for s in range(GROUP):
+            wide_ref[t, PITCH * s : PITCH * s + QUARTER, :] = tile[s]
 
     lane = lax.broadcasted_iota(jnp.int32, (WF, 128), 1)
     row = lax.broadcasted_iota(jnp.int32, (WF, 128), 0)
     eye = lane == row
     fermi = level_ref[0:1, :]
     zero = jnp.zeros((32, 256), bf16)
-    mine = range(PER_STEP)
 
     where = {}
     for c in range(4):
@@ -242,8 +303,8 @@
             at = c * PIECE + r * 2 * WF
             odd = at % 128 != 0
             where[c, r] = (odd, 32 * sum(1 for w in where.values() if w[0] == odd), at // 128)
-    for q in mine:
-        k = step * PER_STEP + q
+
+    def first_product(k, slot):
         for odd, at in ((False, 64), (True, 0)):
             rows = jnp.concatenate(
                 [
@@ -259,75 +320,83 @@
                 ],
                 axis=0,
             )
-            weights = wu_ref[q, at : at + 256, :]
+            weights = wu_ref[k, at : at + 256, :]
             half = jnp.dot(rows, weights, preferred_element_type=f32).astype(bf16)
             for (c, r), w in where.items():
                 if w[0] == odd:
-                    half_ref[q, c, 32 * r : 32 * r + 32, :] = half[w[1] : w[1] + 32]
-    for q in mine:
+                    half_ref[slot, c, 32 * r : 32 * r + 32, :] = half[w[1] : w[1] + 32]
+
+    def second_product(k, slot, bloch_ref):
         for c in range(4):
-            b_re, b_im = hermitian(*rotate(ut_ref[q], half_ref[q, c]))
-            bloch_ref[q, c, :, 0:128] = b_re.astype(bf16)
-            bloch_ref[q, c, :, 128:256] = b_im.astype(bf16)
-    for q in mine:
-        k = step * PER_STEP + q
-        diag = jnp.where(eye, bloch_ref[q, 0, :, 0:128].astype(f32), 0.0)
+            b_re, b_im = hermitian(*rotate(ut_ref[k], half_ref[slot, c]))
+            bloch_ref[c, :, 0:128] = b_re.astype(bf16)
+            bloch_ref[c, :, 128:256] = b_im.astype(bf16)
+
+    sums = [jnp.zeros((1, 128), f32) for _ in range(9)]
+
+    def kubo(k, bloch_ref):
+        diag = jnp.where(eye, bloch_ref[0, :, 0:128].astype(f32), 0.0)
         e_row = jnp.sum(diag, axis=0, keepdims=True)
         e_col = jnp.sum(diag, axis=1, keepdims=True)
         gap = e_col - e_row
         weight = -1.0 / (gap * gap + broadening * broadening)
         occupation = 1.0 / (1.0 + jnp.exp((e_row - fermi) / smearing))
         for a in range(3):
-            v = bloch_ref[q, 1 + a]
+            v = bloch_ref[1 + a]
             v_re, v_im = v[:, 0:128], v[:, 128:256]
             rhs = jnp.concatenate(
                 [v, zero, jnp.concatenate([-v_im, v_re], axis=1), zero], axis=0
             )
-            prod = jnp.dot(sb_ref[q], rhs, preferred_element_type=f32)
+            prod = jnp.dot(sb_ref[k], rhs, preferred_element_type=f32)
             p_re = prod[:, 0:128]
             p_im = prod[:, 128:256]
             c_re = (p_re + flip_square(p_re)) * weight
             c_im = (p_im - flip_square(p_im)) * weight
             for b in range(3):
-                w_re = bloch_ref[q, 1 + b, :, 0:128].astype(f32)
-                w_im = bloch_ref[q, 1 + b, :, 128:256].astype(f32)
+                w_re = bloch_ref[1 + b, :, 0:128].astype(f32)
+                w_im = bloch_ref[1 + b, :, 128:256].astype(f32)
                 curve = jnp.sum(c_re * w_im - c_im * w_re, axis=0, keepdims=True)
-                curve_ref[3 * a + b, pl.ds(k, 1), :] = curve[:, 0:WF]
-                sum_ref[3 * a + b : 3 * a + b + 1, :] += occupation * curve
-
-    @pl.when(step == pl.num_programs(0) - 1)
-    def _():
-        last = jnp.broadcast_to(sum_ref[8:9, :], (8, 128))
-        lane8 = lax.broadcasted_iota(jnp.int32, (8, 128), 1)
-        row8 = lax.broadcasted_iota(jnp.int32, (8, 128), 0)
-        extra = jnp.zeros((8, 128), f32)
-        for t in range(3):
-            extra = jnp.where(row8 == t, pltpu.roll(last, 96 - 32 * t, 1), extra)
-        packed = jnp.where(lane8 < WF, sum_ref[0:8, :], extra)
-        total_ref[...] = jnp.broadcast_to(packed[None], total_ref.shape)
+                curve_ref[3 * a + b, k : k + 1, :] = curve[:, 0:WF]
+                sums[3 * a + b] = sums[3 * a + b] + occupation * curve
+
+    steps = QUARTER // PER_STEP
+    for i in range(steps + 1):
+        for q in range(PER_STEP):
+            if i < steps:
+                first_product(i * PER_STEP + q, i % 2 * PER_STEP + q)
+        for q in range(PER_STEP):
+            if i > 0:
+                kubo((i - 1) * PER_STEP + q, bloch_refs[(i - 1) % 2 * PER_STEP + q])
+            if i < steps:
+                slot = i % 2 * PER_STEP + q
+                second_product(i * PER_STEP + q, slot, bloch_refs[slot])
+
+    lane8 = lax.broadcasted_iota(jnp.int32, (8, 128), 1)
+    row8 = lax.broadcasted_iota(jnp.int32, (8, 128), 0)
+    packed = jnp.zeros((8, 128), f32)
+    for ab in range(8):
+        packed = jnp.where(row8 == ab, sums[ab], packed)
+    last = jnp.broadcast_to(sums[8], (8, 128))
+    for t in range(3):
+        moved = pltpu.roll(last, 96 - 32 * t, 1)
+        packed = jnp.where((lane8 >= WF) & (row8 == t), moved, packed)
+    total_ref[...] = jnp.broadcast_to(packed[None], total_ref.shape)
 
 
 def bands(count, prepared, got, level):
-    per = QUARTER // PER_STEP
     shapes = [(9, QUARTER, WF), (count, 8, 128)]
+    vmem = pl.BlockSpec(memory_space=pltpu.VMEM)
     return pl.pallas_call(
         bands_kernel,
-        grid=(per,),
-        in_specs=[
-            pl.BlockSpec((PER_STEP, *p.shape[1:]), lambda i: (i, 0, 0)) for p in prepared
-        ]
-        + [pl.BlockSpec(memory_space=pltpu.VMEM)] * 2,
-        out_specs=[pl.BlockSpec(memory_space=pltpu.VMEM) for _ in shapes],
+        in_specs=[vmem] * 5,
+        out_specs=[vmem] * 2,
         out_shape=[jax.ShapeDtypeStruct(shape, f32) for shape in shapes],
         scratch_shapes=[
             pltpu.VMEM((KEPT // 128, GROUP * PITCH, 128), f32),
-            pltpu.VMEM((PER_STEP, 4, WF, 256), bf16),
-            pltpu.VMEM((PER_STEP, 4, WF, 256), bf16),
-            pltpu.VMEM((16, 128), f32),
-        ],
-        compiler_params=pltpu.CompilerParams(
-            dimension_semantics=("arbitrary",), vmem_limit_bytes=30 << 20
-        ),
+            pltpu.VMEM((2 * PER_STEP, 4, WF, 256), bf16),
+        ]
+        + [pltpu.VMEM((4, WF, 256), bf16)] * (2 * PER_STEP),
+        compiler_params=pltpu.CompilerParams(vmem_limit_bytes=30 << 20),
         name="bands",
     )(*prepared, got, level)
 
@@ -338,17 +407,12 @@
 
 def on_device(hamiltonian, eigvecs, spin, k_indices, r_vectors, degeneracy, fermi_level):
     own = hamiltonian.shape[0]
-    pieces = hamiltonian.reshape(own, 2, ROWS, GROUP, WF).transpose(3, 0, 2, 1, 4)
-    pieces = pieces.reshape(GROUP, own, PIECE)
-    points = jnp.zeros((own, WIDE - PIECE), bf16).at[0:3, :].set(k_indices.T.astype(bf16))
-    points = jnp.broadcast_to(points[None], (GROUP, own, WIDE - PIECE))
-    pieces = jnp.concatenate([pieces, points], axis=2)
-    pieces = jnp.broadcast_to(pieces[None], (4, GROUP, own, WIDE)).reshape(4 * GROUP, own, WIDE)
+    count = lax.axis_size("z") * lax.axis_size("y") * lax.axis_size("core") * lax.axis_size("x")
+    pieces = pack(hamiltonian, k_indices.T, count)
     hopping = exchange(pieces, ALL)
     column = lax.axis_index("x").astype(jnp.int32).reshape(1)
     vectors = pltpu.with_memory_space_constraint(eigvecs, pltpu.HBM)
     *prepared, level = sides(column, vectors, spin, fermi_level.reshape(1, 1))
-    prepared = [pltpu.with_memory_space_constraint(p, pltpu.HBM) for p in prepared]
     layer = lax.axis_index("z")
     mine = lax.dynamic_slice(hopping, (layer * GROUP, 0, 0), (GROUP, own, WIDE))
     k_rows = mine.reshape(8, 4, own, WIDE)[:, 0, :, PIECE:]
@@ -359,7 +423,6 @@
     entries = interpolate(k_rows, lattice, hopping.reshape(NR, WIDE))
     entries, level, *prepared = lax.optimization_barrier((entries, level, *prepared))
     got = exchange(entries, PLANE)
-    count = lax.axis_size("z") * lax.axis_size("y") * lax.axis_size("core") * lax.axis_size("x")
     curvature, copies = bands(count, prepared, got, level)
     total_points = k_indices.shape[0] * count // 4
     total = jnp.sum(exchange(copies, ALL), axis=0) * (1.0 / math.sqrt(total_points))

time: 111 us -> 106 us (0.955)
  local copies, waits for them, and re-layouts: 6.75 us -> 1.85 us
  waiting for transfers between devices: 12.9 us -> 14.7 us
    reshape x3 -> x0, local copies, waits for them, and re-layouts: 1.93 us -> none  [the longest x2 1.61 us: on_device(): hamiltonian.reshape(own, 2, ROWS, GROUP, WF).transpose(3, 0, 2, 1, 4)]
    all_to_all x1, waiting for transfers between devices: 12.9 us -> 14.7 us  [exchange(): return lax.all_to_all(value, axes, split_axis=0, concat_axis=0, tiled=True)]
    unnamed x12 -> x10, local copies, waits for them, and re-layouts: 3.33 us -> 1.54 us
    broadcast_in_dim x2 -> x0, local copies, waits for them, and re-layouts: 1.17 us -> none  [the longest x1 1.16 us: on_device(): jnp.broadcast_to(pieces[None], (4, GROUP, own, WIDE))]
    pallas_call x1 -> x2, Pallas kernels: 9.97 us -> 9.11 us  [the longest x1 6.34 us: bands(): pl.pallas_call(bands_kernel, in_specs=[vmem] * 5, out_specs=[vmem] * 2, o...]
where the time goes in v3:
time: 106 us
  blocking collectives  52.8 us (50%)
  Pallas kernels  22.8 us (22%)
  waiting for transfers between devices  14.7 us (14%)
  starting transfers between devices  11.5 us (11%)
  local copies, waits for them, and re-layouts  1.85 us (2%)
  between operations  1.41 us (1%)
    all_to_all x2, blocking collectives, exchange(): return lax.all_to_all(value, axes, split_axis=0, concat_axis=0, tiled=True)  52.8 us
    all_to_all x1, waiting for transfers between devices, exchange(): return lax.all_to_all(value, axes, split_axis=0, concat_axis=0, tiled=True)  14.7 us
    all_to_all x1, starting transfers between devices, exchange(): return lax.all_to_all(value, axes, split_axis=0, concat_axis=0, tiled=True)  11.5 us
    pallas_call x1, Pallas kernels, interpolate(): pl.pallas_call(interpolate_kernel, in_specs=[vmem, vmem, vmem], out_specs...  8.34 us
    pallas_call x1, Pallas kernels, bands(): pl.pallas_call(bands_kernel, in_specs=[vmem] * 5, out_specs=[vmem] * 2, o...  6.34 us
    pallas_call x1, Pallas kernels, sides(): pl.pallas_call(sides_kernel, grid_spec=grid_spec, out_shape=[jax.ShapeDty...  5.38 us
    pallas_call x1, Pallas kernels, pack(): pl.pallas_call(pack_kernel, in_specs=[vmem, vmem], out_specs=pl.BlockSpec...  2.77 us
  transfers between devices with their start and end apart: 1, of which 1 were waited for; matrix products, arithmetic and copies ran while one was open for 0% of the time, Pallas kernels for 5%

profile of v3, /device:TPU:1, one launch (start us, length us, event | category | flops | bytes accessed | tf_op | source)
XLA Modules:
  0.0 105.9 jit_solution(10765433458484502198)
XLA Ops:
  0.6 0.0 copy-start.4
  0.6 0.0 copy-start.2
  0.7 2.8 %pack.1 = bf16[128,8,640]{2,1,0:T(8,128)(2,1)} custom-call(bf16[8,2,9216]{2,1,0:T(2,128)(2,1)} %ham_ref.1, s32[3,64]{1,0:T(4,128)} %bitcast.22), custom_call_target="tpu_custom_call" | custom-call | tf_op jit(solution)/shard_map/pack/pallas_call | solution.py:117
  3.4 11.5 %all-to-all-start = ((bf16[128,8,640]{2,1,0:T(8,128)(2,1)}), bf16[128,8,640]{2,1,0:T(8,128)(2,1)S(1)}, u32[]{:S(2)}, u32[]{:S(2)}) async-start(bf16[128,8,640]{2,1,0:T(8,128)(2,1)} %pack.1), calls=%async_computation | async-start | bytes 2621440 | tf_op jit(solution)/shard_map/all_to_all | solution.py:405
  14.9 0.0 copy-start.3
  15.6 0.0 copy-done.4
  15.6 0.0 copy-done.2
  15.6 5.4 %sides.1 = (bf16[16,320,256]{2,1,0:T(8,128)(2,1)S(1)}, bf16[16,96,256]{2,1,0:T(8,128)(2,1)S(1)}, bf16[16,96,256]{2,1,0:T(8,128)(2,1)S(1)}, f32[8,128]{1,0:T(8,128)S(1)}) custom-call(s32[1]{0:T(128)} %bitcast.7.column_ref, bf16[64,2,96,96]{3,2,1,0:T(8,128)(2,1)} %vec_ref.1, bf16[2,96,96]{2,1,0:T(8,128)(2,1)S(1)} %copy-done.2, f32[1,1]{1,0:T(1,128)} %bitcast.17.fermi_ref), custom_call_target="tpu_custom_call" | custom-call | flops 1073741824 | bytes 5767168 | tf_op jit(solution)/shard_map/sides/pallas_call | solution.py:268
  21.0 0.0 copy-start
  21.0 1.5 %copy-done = bf16[16,320,256]{2,1,0:T(8,128)(2,1)} copy-done((bf16[16,320,256]{2,1,0:T(8,128)(2,1)}, bf16[16,320,256]{2,1,0:T(8,128)(2,1)S(1)}, u32[]{:S(2)}) %copy-start) | copy-done | bytes 2621464
  22.5 0.0 copy-done.3
  22.6 14.7 %all-to-all-done = bf16[128,8,640]{2,1,0:T(8,128)(2,1)S(1)} async-done(((bf16[128,8,640]{2,1,0:T(8,128)(2,1)}), bf16[128,8,640]{2,1,0:T(8,128)(2,1)S(1)}, u32[]{:S(2)}, u32[]{:S(2)}) %all-to-all-start) | async-done | bytes 1310752 | tf_op jit(solution)/shard_map/all_to_all | solution.py:405
  37.3 0.1 convert_bitcast_fusion
  37.4 0.1 copy.9
  37.5 8.3 %interpolate.1 = bf16[32,16,2304]{2,1,0:T(8,128)(2,1)S(1)} custom-call(f32[512,8]{1,0:T(8,128)S(1)} %bitcast.19, f32[8,1024]{1,0:T(8,128)S(1)} %pad_maximum_fusion.lat_ref, bf16[1024,640]{1,0:T(8,128)(2,1)S(1)} %bitcast.18), custom_call_target="tpu_custom_call" | custom-call | tf_op jit(solution)/shard_map/interpolate/pallas_call | solution.py:196
  45.9 0.0 copy-start.1
  45.9 34.8 %all_to_all.15.got_ref = bf16[32,16,2304]{2,1,0:T(8,128)(2,1)S(1)} all-to-all(bf16[32,16,2304]{2,1,0:T(8,128)(2,1)S(1)} %interpolate.1), channel_id=1, replica_groups=mesh['z'=4,'y'=4,'core'=2,'x'=4] {'y','core','x'}, dimensions={0} | all-to-all | bytes 4718592 | tf_op jit(solution)/shard_map/all_to_all | solution.py:405
  80.7 0.0 copy-done.1
  80.7 6.3 %bands.1 = (f32[9,16,96]{2,1,0:T(8,128)}, f32[128,8,128]{2,1,0:T(8,128)S(1)}) custom-call(bf16[16,320,256]{2,1,0:T(8,128)(2,1)S(1)} %copy-done.1, bf16[16,96,256]{2,1,0:T(8,128)(2,1)S(1)} %get-tuple-element.18.ut_ref, bf16[16,96,256]{2,1,0:T(8,128)(2,1)S(1)} %get-tuple-element.19.sb_ref, bf16[32,16,2304]{2,1,0:T(8,128)(2,1)S(1)} %all_to_all.15.got_ref, ...), custom_call_target="tpu_custom_call" | custom-call | tf_op jit(solution)/shard_map/bands/pallas_call | solution.py:389
  87.0 18.0 %all_to_all.16 = f32[128,8,128]{2,1,0:T(8,128)S(1)} all-to-all(f32[128,8,128]{2,1,0:T(8,128)S(1)} %get-tuple-element.23), channel_id=1, replica_groups=mesh['z'=4,'y'=4,'core'=2,'x'=4] {'z','y','core','x'}, dimensions={0} | all-to-all | bytes 1048576 | tf_op jit(solution)/shard_map/all_to_all | solution.py:405
  105.0 0.1 reduce_sum.9
  105.1 0.1 slice.11
  105.2 0.1 reshape.29
  105.3 0.6 pad_maximum_fusion.1
  (6 shorter events, 0.1 us)
Async XLA Ops:
  0.6 15.0 %copy-start.4 = (s32[1024]{0:T(1024)S(1)}, s32[1024]{0:T(1024)}, u32[]{:S(2)}) copy-start(s32[1024]{0:T(1024)} %param.12) | copy-start | bytes 12292
  0.6 15.0 %copy-start.2 = (bf16[2,96,96]{2,1,0:T(8,128)(2,1)S(1)}, bf16[2,96,96]{2,1,0:T(8,128)(2,1)}, u32[]{:S(2)}) copy-start(bf16[2,96,96]{2,1,0:T(8,128)(2,1)} %spin_ref.1) | copy-start | bytes 110596
  3.4 33.8 %all-to-all-start = ((bf16[128,8,640]{2,1,0:T(8,128)(2,1)}), bf16[128,8,640]{2,1,0:T(8,128)(2,1)S(1)}, u32[]{:S(2)}, u32[]{:S(2)}) async-start(bf16[128,8,640]{2,1,0:T(8,128)(2,1)} %pack.1), calls=%async_computation | async-start | bytes 2621440 | tf_op jit(solution)/shard_map/all_to_all | solution.py:405
  14.9 7.6 %copy-start.3 = (s32[1024,3]{0,1:T(4,128)S(1)}, s32[1024,3]{0,1:T(4,128)}, u32[]{:S(2)}) copy-start(s32[1024,3]{0,1:T(4,128)} %param.11) | copy-start | bytes 36868
  21.0 1.5 %copy-start = (bf16[16,320,256]{2,1,0:T(8,128)(2,1)}, bf16[16,320,256]{2,1,0:T(8,128)(2,1)S(1)}, u32[]{:S(2)}) copy-start(bf16[16,320,256]{2,1,0:T(8,128)(2,1)S(1)} %get-tuple-element.17.wu_ref) | copy-start | bytes 7864324
  45.9 34.8 %copy-start.1 = (bf16[16,320,256]{2,1,0:T(8,128)(2,1)S(1)}, bf16[16,320,256]{2,1,0:T(8,128)(2,1)}, u32[]{:S(2)}) copy-start(bf16[16,320,256]{2,1,0:T(8,128)(2,1)} %copy-done) | copy-start | bytes 7864324

commit v4 on v3

--- a/solution.py
+++ b/solution.py
@@ -67,6 +67,7 @@
     points_ref[0:3, 64:128] = k_ref[...].astype(f32)
     points = points_ref[...]
     loaded = {}
+    copies = []
 
     def tile(part, t):
         if (part, t) not in loaded:
@@ -100,13 +101,16 @@
                 other = segment(right[0], GROUP * right[1] + g, *right[2:])
             value = jnp.where(lane < size, value, other)
             piece_ref[g, :, 128 * t : 128 * (t + 1)] = value.astype(bf16)
-    layers = out_ref.shape[0] // GROUP
-    copies = [
-        pltpu.make_async_copy(piece_ref, out_ref.at[pl.ds(GROUP * z, GROUP)], sems.at[z])
-        for z in range(layers)
-    ]
-    for copy in copies:
-        copy.start()
+        if g % 8 == 7:
+            for z in range(out_ref.shape[0] // GROUP):
+                copies.append(
+                    pltpu.make_async_copy(
+                        piece_ref.at[pl.ds(g - 7, 8)],
+                        out_ref.at[pl.ds(GROUP * z + g - 7, 8)],
+                        sems.at[g // 8, z],
+                    )
+                )
+                copies[-1].start()
     for copy in copies:
         copy.wait()
 
@@ -122,7 +126,7 @@
         scratch_shapes=[
             pltpu.VMEM((GROUP, own, WIDE), bf16),
             pltpu.VMEM((8, 128), f32),
-            pltpu.SemaphoreType.DMA((count // GROUP,)),
+            pltpu.SemaphoreType.DMA((4, count // GROUP)),
         ],
         name="pack",
     )(hamiltonian, k_rows)
@@ -131,24 +135,22 @@
 def turn_hopping(hop_ref, w_ref):
     lane = lax.broadcasted_iota(jnp.int32, (NR, 128), 1)
     tiles = [hop_ref[:, 128 * t : 128 * (t + 1)].astype(f32) for t in range(5)]
-    tiles[4] = jnp.where(lane < 64, tiles[4], 0.0)
     ups = [pltpu.roll(t, 96, 1) for t in tiles]
     downs = [pltpu.roll(t, 32, 1) for t in tiles]
     for t in range(5):
-        w_ref[0:NR, 128 * t : 128 * (t + 1)] = tiles[t].astype(bf16)
         up = jnp.where(lane < 96, ups[(t - 1) % 5], ups[t])
         down = jnp.where(lane < 32, downs[t], downs[(t + 1) % 5])
         place = (lane + 128 * t) % (2 * WF)
         turned = jnp.where(place < WF, -down, up)
-        if t == 4:
-            turned = jnp.where(lane < 64, turned, 0.0)
-        w_ref[NR : 2 * NR, 128 * t : 128 * (t + 1)] = turned.astype(bf16)
+        w_ref[:, 128 * t : 128 * (t + 1)] = turned.astype(bf16)
 
 
 def phase_block(k, lat_ref, p_ref):
     r = [lat_ref[a : a + 1, :] for a in range(3)]
     inverse = 1.0 / lat_ref[3:4, :]
-    turns = sum(k[:, a : a + 1] * (r[a] * (1.0 / GRID)) for a in range(3))
+    turns = jnp.dot(
+        k.astype(bf16), (lat_ref[...] * (1.0 / GRID)).astype(bf16), preferred_element_type=f32
+    )
     cosine, sine = turn(turns - jnp.floor(turns + 0.5))
     for c in range(4):
         rows = slice(c * STEP_K, (c + 1) * STEP_K)
@@ -174,7 +176,9 @@
     for i in range(steps):
         if i + 1 < steps:
             phases(i + 1)
-        summed = jnp.dot(p_refs[i % 2][...], w_ref[...], preferred_element_type=f32)
+        p_ref = p_refs[i % 2]
+        summed = jnp.dot(p_ref[:, 0:NR], hop_ref[...], preferred_element_type=f32)
+        summed += jnp.dot(p_ref[:, NR : 2 * NR], w_ref[...], preferred_element_type=f32)
         for pair in range(2):
             even = summed[2 * pair * STEP_K : (2 * pair + 1) * STEP_K]
             odd = summed[(2 * pair + 1) * STEP_K : (2 * pair + 2) * STEP_K]
@@ -199,7 +203,7 @@
         out_specs=vmem,
         out_shape=jax.ShapeDtypeStruct((GROUP, QUARTER, KEPT), bf16),
         scratch_shapes=[
-            pltpu.VMEM((2 * NR, WIDE), bf16),
+            pltpu.VMEM((NR, WIDE), bf16),
             pltpu.VMEM((4 * STEP_K, 2 * NR), bf16),
             pltpu.VMEM((4 * STEP_K, 2 * NR), bf16),
         ],
@@ -284,8 +288,9 @@
 
 def bands_kernel(
     wu_ref, ut_ref, sb_ref, got_ref, level_ref, curve_ref, total_ref,
-    wide_ref, half_ref, *bloch_refs,
+    wide_ref, half_ref, *others,
 ):
+    bloch_refs, flow_refs = others[: 2 * PER_STEP], others[2 * PER_STEP :]
     for t in range(KEPT // 128):
         tile = got_ref[:, :, 128 * t : 128 * (t + 1)].astype(f32)
         for s in range(GROUP):
@@ -334,13 +339,7 @@
 
     sums = [jnp.zeros((1, 128), f32) for _ in range(9)]
 
-    def kubo(k, bloch_ref):
-        diag = jnp.where(eye, bloch_ref[0, :, 0:128].astype(f32), 0.0)
-        e_row = jnp.sum(diag, axis=0, keepdims=True)
-        e_col = jnp.sum(diag, axis=1, keepdims=True)
-        gap = e_col - e_row
-        weight = -1.0 / (gap * gap + broadening * broadening)
-        occupation = 1.0 / (1.0 + jnp.exp((e_row - fermi) / smearing))
+    def currents(k, bloch_ref, flow_ref):
         for a in range(3):
             v = bloch_ref[1 + a]
             v_re, v_im = v[:, 0:128], v[:, 128:256]
@@ -350,14 +349,34 @@
             prod = jnp.dot(sb_ref[k], rhs, preferred_element_type=f32)
             p_re = prod[:, 0:128]
             p_im = prod[:, 128:256]
-            c_re = (p_re + flip_square(p_re)) * weight
-            c_im = (p_im - flip_square(p_im)) * weight
-            for b in range(3):
-                w_re = bloch_ref[1 + b, :, 0:128].astype(f32)
-                w_im = bloch_ref[1 + b, :, 128:256].astype(f32)
-                curve = jnp.sum(c_re * w_im - c_im * w_re, axis=0, keepdims=True)
-                curve_ref[3 * a + b, k : k + 1, :] = curve[:, 0:WF]
-                sums[3 * a + b] = sums[3 * a + b] + occupation * curve
+            flow_ref[a, :, 0:128] = p_re + flip_square(p_re)
+            flow_ref[a, :, 128:256] = p_im - flip_square(p_im)
+
+    def kubo(k, bloch_ref, flow_ref):
+        diag = jnp.where(eye, bloch_ref[0, :, 0:128].astype(f32), 0.0)
+        e_row = jnp.sum(diag, axis=0, keepdims=True)
+        e_col = jnp.sum(diag, axis=1, keepdims=True)
+        occupation = 1.0 / (1.0 + jnp.exp((e_row - fermi) / smearing))
+        parts = [None] * 9
+        for at in range(0, WF, 16):
+            rows = slice(at, at + 16)
+            gap = e_col[rows] - e_row
+            weight = -1.0 / (gap * gap + broadening * broadening)
+            v = [
+                [bloch_ref[1 + b, rows, 128 * p : 128 * (p + 1)].astype(f32) for p in range(2)]
+                for b in range(3)
+            ]
+            for a in range(3):
+                c_re = flow_ref[a, rows, 0:128] * weight
+                c_im = flow_ref[a, rows, 128:256] * weight
+                for b in range(3):
+                    term = c_re * v[b][1] - c_im * v[b][0]
+                    ab = 3 * a + b
+                    parts[ab] = term if parts[ab] is None else parts[ab] + term
+        for ab in range(9):
+            curve = jnp.sum(parts[ab], axis=0, keepdims=True)
+            curve_ref[ab, k : k + 1, :] = curve[:, 0:WF]
+            sums[ab] = sums[ab] + occupation * curve
 
     steps = QUARTER // PER_STEP
     for i in range(steps + 1):
@@ -366,7 +385,9 @@
                 first_product(i * PER_STEP + q, i % 2 * PER_STEP + q)
         for q in range(PER_STEP):
             if i > 0:
-                kubo((i - 1) * PER_STEP + q, bloch_refs[(i - 1) % 2 * PER_STEP + q])
+                before = (i - 1) % 2 * PER_STEP + q
+                currents((i - 1) * PER_STEP + q, bloch_refs[before], flow_refs[q])
+                kubo((i - 1) * PER_STEP + q, bloch_refs[before], flow_refs[q])
             if i < steps:
                 slot = i % 2 * PER_STEP + q
                 second_product(i * PER_STEP + q, slot, bloch_refs[slot])
@@ -395,7 +416,8 @@
             pltpu.VMEM((KEPT // 128, GROUP * PITCH, 128), f32),
             pltpu.VMEM((2 * PER_STEP, 4, WF, 256), bf16),
         ]
-        + [pltpu.VMEM((4, WF, 256), bf16)] * (2 * PER_STEP),
+        + [pltpu.VMEM((4, WF, 256), bf16)] * (2 * PER_STEP)
+        + [pltpu.VMEM((3, WF, 256), f32)] * PER_STEP,
         compiler_params=pltpu.CompilerParams(vmem_limit_bytes=30 << 20),
         name="bands",
     )(*prepared, got, level)

time: 106 us -> 106 us (level)
  no operation moved by 1% of the time
where the time goes in v4:
time: 106 us
  blocking collectives  52.8 us (50%)
  Pallas kernels  22.6 us (21%)
  waiting for transfers between devices  14.7 us (14%)
  starting transfers between devices  11.5 us (11%)
  local copies, waits for them, and re-layouts  1.85 us (2%)
  between operations  1.41 us (1%)
    all_to_all x2, blocking collectives, exchange(): return lax.all_to_all(value, axes, split_axis=0, concat_axis=0, tiled=True)  52.8 us
    all_to_all x1, waiting for transfers between devices, exchange(): return lax.all_to_all(value, axes, split_axis=0, concat_axis=0, tiled=True)  14.7 us
    all_to_all x1, starting transfers between devices, exchange(): return lax.all_to_all(value, axes, split_axis=0, concat_axis=0, tiled=True)  11.5 us
    pallas_call x1, Pallas kernels, interpolate(): pl.pallas_call(interpolate_kernel, in_specs=[vmem, vmem, vmem], out_specs...  8.34 us
    pallas_call x1, Pallas kernels, bands(): pl.pallas_call(bands_kernel, in_specs=[vmem] * 5, out_specs=[vmem] * 2, o...  6.19 us
    pallas_call x1, Pallas kernels, sides(): pl.pallas_call(sides_kernel, grid_spec=grid_spec, out_shape=[jax.ShapeDty...  5.38 us
    pallas_call x1, Pallas kernels, pack(): pl.pallas_call(pack_kernel, in_specs=[vmem, vmem], out_specs=pl.BlockSpec...  2.72 us
  transfers between devices with their start and end apart: 1, of which 1 were waited for; matrix products, arithmetic and copies ran while one was open for 0% of the time, Pallas kernels for 5%

profile of v4, /device:TPU:1, one launch (start us, length us, event | category | flops | bytes accessed | tf_op | source)
XLA Modules:
  0.0 105.7 jit_solution(11067603886438250422)
XLA Ops:
  0.6 0.0 copy-start.4
  0.6 0.0 copy-start.2
  0.7 2.7 %pack.1 = bf16[128,8,640]{2,1,0:T(8,128)(2,1)} custom-call(bf16[8,2,9216]{2,1,0:T(2,128)(2,1)} %ham_ref.1, s32[3,64]{1,0:T(4,128)} %bitcast.22), custom_call_target="tpu_custom_call" | custom-call | tf_op jit(solution)/shard_map/pack/pallas_call | solution.py:121
  3.4 11.5 %all-to-all-start = ((bf16[128,8,640]{2,1,0:T(8,128)(2,1)}), bf16[128,8,640]{2,1,0:T(8,128)(2,1)S(1)}, u32[]{:S(2)}, u32[]{:S(2)}) async-start(bf16[128,8,640]{2,1,0:T(8,128)(2,1)} %pack.1), calls=%async_computation | async-start | bytes 2621440 | tf_op jit(solution)/shard_map/all_to_all | solution.py:427
  14.9 0.0 copy-start.3
  15.5 0.0 copy-done.4
  15.6 0.0 copy-done.2
  15.6 5.4 %sides.1 = (bf16[16,320,256]{2,1,0:T(8,128)(2,1)S(1)}, bf16[16,96,256]{2,1,0:T(8,128)(2,1)S(1)}, bf16[16,96,256]{2,1,0:T(8,128)(2,1)S(1)}, f32[8,128]{1,0:T(8,128)S(1)}) custom-call(s32[1]{0:T(128)} %bitcast.7.column_ref, bf16[64,2,96,96]{3,2,1,0:T(8,128)(2,1)} %vec_ref.1, bf16[2,96,96]{2,1,0:T(8,128)(2,1)S(1)} %copy-done.2, f32[1,1]{1,0:T(1,128)} %bitcast.17.fermi_ref), custom_call_target="tpu_custom_call" | custom-call | flops 1073741824 | bytes 5767168 | tf_op jit(solution)/shard_map/sides/pallas_call | solution.py:272
  21.0 0.0 copy-start
  21.0 1.5 %copy-done = bf16[16,320,256]{2,1,0:T(8,128)(2,1)} copy-done((bf16[16,320,256]{2,1,0:T(8,128)(2,1)}, bf16[16,320,256]{2,1,0:T(8,128)(2,1)S(1)}, u32[]{:S(2)}) %copy-start) | copy-done | bytes 2621464
  22.5 0.0 copy-done.3
  22.5 14.7 %all-to-all-done = bf16[128,8,640]{2,1,0:T(8,128)(2,1)S(1)} async-done(((bf16[128,8,640]{2,1,0:T(8,128)(2,1)}), bf16[128,8,640]{2,1,0:T(8,128)(2,1)S(1)}, u32[]{:S(2)}, u32[]{:S(2)}) %all-to-all-start) | async-done | bytes 1310752 | tf_op jit(solution)/shard_map/all_to_all | solution.py:427
  37.2 0.1 convert_bitcast_fusion
  37.3 0.1 copy.9
  37.5 8.3 %interpolate.1 = bf16[32,16,2304]{2,1,0:T(8,128)(2,1)S(1)} custom-call(f32[512,8]{1,0:T(8,128)S(1)} %bitcast.19, f32[8,1024]{1,0:T(8,128)S(1)} %pad_maximum_fusion.lat_ref, bf16[1024,640]{1,0:T(8,128)(2,1)S(1)} %bitcast.18), custom_call_target="tpu_custom_call" | custom-call | tf_op jit(solution)/shard_map/interpolate/pallas_call | solution.py:200
  45.8 0.0 copy-start.1
  45.8 34.8 %all_to_all.15.got_ref = bf16[32,16,2304]{2,1,0:T(8,128)(2,1)S(1)} all-to-all(bf16[32,16,2304]{2,1,0:T(8,128)(2,1)S(1)} %interpolate.1), channel_id=1, replica_groups=mesh['z'=4,'y'=4,'core'=2,'x'=4] {'y','core','x'}, dimensions={0} | all-to-all | bytes 4718592 | tf_op jit(solution)/shard_map/all_to_all | solution.py:427
  80.6 0.0 copy-done.1
  80.6 6.2 %bands.1 = (f32[9,16,96]{2,1,0:T(8,128)}, f32[128,8,128]{2,1,0:T(8,128)S(1)}) custom-call(bf16[16,320,256]{2,1,0:T(8,128)(2,1)S(1)} %copy-done.1, bf16[16,96,256]{2,1,0:T(8,128)(2,1)S(1)} %get-tuple-element.18.ut_ref, bf16[16,96,256]{2,1,0:T(8,128)(2,1)S(1)} %get-tuple-element.19.sb_ref, bf16[32,16,2304]{2,1,0:T(8,128)(2,1)S(1)} %all_to_all.15.got_ref, ...), custom_call_target="tpu_custom_call" | custom-call | tf_op jit(solution)/shard_map/bands/pallas_call | solution.py:410
  86.8 18.0 %all_to_all.16 = f32[128,8,128]{2,1,0:T(8,128)S(1)} all-to-all(f32[128,8,128]{2,1,0:T(8,128)S(1)} %get-tuple-element.23), channel_id=1, replica_groups=mesh['z'=4,'y'=4,'core'=2,'x'=4] {'z','y','core','x'}, dimensions={0} | all-to-all | bytes 1048576 | tf_op jit(solution)/shard_map/all_to_all | solution.py:427
  104.8 0.1 reduce_sum.9
  104.9 0.1 slice.11
  105.0 0.1 reshape.29
  105.1 0.6 pad_maximum_fusion.1
  (6 shorter events, 0.1 us)
Async XLA Ops:
  0.6 14.9 %copy-start.4 = (s32[1024]{0:T(1024)S(1)}, s32[1024]{0:T(1024)}, u32[]{:S(2)}) copy-start(s32[1024]{0:T(1024)} %param.12) | copy-start | bytes 12292
  0.6 14.9 %copy-start.2 = (bf16[2,96,96]{2,1,0:T(8,128)(2,1)S(1)}, bf16[2,96,96]{2,1,0:T(8,128)(2,1)}, u32[]{:S(2)}) copy-start(bf16[2,96,96]{2,1,0:T(8,128)(2,1)} %spin_ref.1) | copy-start | bytes 110596
  3.4 33.8 %all-to-all-start = ((bf16[128,8,640]{2,1,0:T(8,128)(2,1)}), bf16[128,8,640]{2,1,0:T(8,128)(2,1)S(1)}, u32[]{:S(2)}, u32[]{:S(2)}) async-start(bf16[128,8,640]{2,1,0:T(8,128)(2,1)} %pack.1), calls=%async_computation | async-start | bytes 2621440 | tf_op jit(solution)/shard_map/all_to_all | solution.py:427
  14.9 7.6 %copy-start.3 = (s32[1024,3]{0,1:T(4,128)S(1)}, s32[1024,3]{0,1:T(4,128)}, u32[]{:S(2)}) copy-start(s32[1024,3]{0,1:T(4,128)} %param.11) | copy-start | bytes 36868
  21.0 1.5 %copy-start = (bf16[16,320,256]{2,1,0:T(8,128)(2,1)}, bf16[16,320,256]{2,1,0:T(8,128)(2,1)S(1)}, u32[]{:S(2)}) copy-start(bf16[16,320,256]{2,1,0:T(8,128)(2,1)S(1)} %get-tuple-element.17.wu_ref) | copy-start | bytes 7864324
  45.8 34.8 %copy-start.1 = (bf16[16,320,256]{2,1,0:T(8,128)(2,1)S(1)}, bf16[16,320,256]{2,1,0:T(8,128)(2,1)}, u32[]{:S(2)}) copy-start(bf16[16,320,256]{2,1,0:T(8,128)(2,1)} %copy-done) | copy-start | bytes 7864324

commit v5 on v4

--- a/solution.py
+++ b/solution.py
@@ -423,6 +423,29 @@
     )(*prepared, got, level)
 
 
+def total_sums(parts, scale):
+    def kernel(parts_ref, out_ref):
+        total = jnp.sum(parts_ref[...], axis=0) * scale
+        out_ref[0:8, :] = total[:, 0:WF]
+        lane = lax.broadcasted_iota(jnp.int32, (8, 128), 1)
+        row = lax.broadcasted_iota(jnp.int32, (8, 128), 0)
+        last = jnp.zeros((8, 128), f32)
+        for t in range(3):
+            moved = pltpu.roll(total, 32 + 32 * t, 1)
+            keep = (row == t) & (lane >= 32 * t) & (lane < 32 * (t + 1))
+            last = jnp.where(keep, moved, last)
+        out_ref[8:9, :] = jnp.sum(last, axis=0, keepdims=True)[:, 0:WF]
+
+    vmem = pl.BlockSpec(memory_space=pltpu.VMEM)
+    return pl.pallas_call(
+        kernel,
+        in_specs=[vmem],
+        out_specs=vmem,
+        out_shape=jax.ShapeDtypeStruct((9, WF), f32),
+        name="total_sums",
+    )(parts)
+
+
 def exchange(value, axes):
     return lax.all_to_all(value, axes, split_axis=0, concat_axis=0, tiled=True)
 
@@ -447,9 +470,7 @@
     got = exchange(entries, PLANE)
     curvature, copies = bands(count, prepared, got, level)
     total_points = k_indices.shape[0] * count // 4
-    total = jnp.sum(exchange(copies, ALL), axis=0) * (1.0 / math.sqrt(total_points))
-    last = total[0:3, WF:].reshape(1, WF)
-    totals = jnp.concatenate([total[:, :WF], last], axis=0)
+    totals = total_sums(exchange(copies, ALL), 1.0 / math.sqrt(total_points))
     return (curvature.transpose(0, 2, 1), totals)
 
 

time: 106 us -> 107 us (level)
  Pallas kernels: 22.6 us -> 24.5 us
    pallas_call x0 -> x1, Pallas kernels: none -> 1.85 us  [total_sums(): pl.pallas_call(kernel, in_specs=[vmem], out_specs=vmem, out_shape=jax.Sha...]
where the time goes in v5:
time: 107 us
  blocking collectives  52.9 us (49%)
  Pallas kernels  24.5 us (23%)
  waiting for transfers between devices  14.7 us (14%)
  starting transfers between devices  11.5 us (11%)
  local copies, waits for them, and re-layouts  1.68 us (2%)
  between operations  1.41 us (1%)
    all_to_all x2, blocking collectives, exchange(): return lax.all_to_all(value, axes, split_axis=0, concat_axis=0, tiled=True)  52.9 us
    all_to_all x1, waiting for transfers between devices, exchange(): return lax.all_to_all(value, axes, split_axis=0, concat_axis=0, tiled=True)  14.7 us
    all_to_all x1, starting transfers between devices, exchange(): return lax.all_to_all(value, axes, split_axis=0, concat_axis=0, tiled=True)  11.5 us
    pallas_call x1, Pallas kernels, interpolate(): pl.pallas_call(interpolate_kernel, in_specs=[vmem, vmem, vmem], out_specs...  8.34 us
    pallas_call x1, Pallas kernels, bands(): pl.pallas_call(bands_kernel, in_specs=[vmem] * 5, out_specs=[vmem] * 2, o...  6.2 us
    pallas_call x1, Pallas kernels, sides(): pl.pallas_call(sides_kernel, grid_spec=grid_spec, out_shape=[jax.ShapeDty...  5.38 us
    pallas_call x1, Pallas kernels, pack(): pl.pallas_call(pack_kernel, in_specs=[vmem, vmem], out_specs=pl.BlockSpec...  2.7 us
  transfers between devices with their start and end apart: 1, of which 1 were waited for; matrix products, arithmetic and copies ran while one was open for 0% of the time, Pallas kernels for 5%

profile of v5, /device:TPU:1, one launch (start us, length us, event | category | flops | bytes accessed | tf_op | source)
XLA Modules:
  0.0 106.7 jit_solution(12267789618944067179)
XLA Ops:
  0.6 0.0 copy-start.4
  0.6 0.0 copy-start.2
  0.7 2.7 %pack.1 = bf16[128,8,640]{2,1,0:T(8,128)(2,1)} custom-call(bf16[8,2,9216]{2,1,0:T(2,128)(2,1)} %ham_ref.1, s32[3,64]{1,0:T(4,128)} %bitcast.20), custom_call_target="tpu_custom_call" | custom-call | tf_op jit(solution)/shard_map/pack/pallas_call | solution.py:121
  3.4 11.5 %all-to-all-start = ((bf16[128,8,640]{2,1,0:T(8,128)(2,1)}), bf16[128,8,640]{2,1,0:T(8,128)(2,1)S(1)}, u32[]{:S(2)}, u32[]{:S(2)}) async-start(bf16[128,8,640]{2,1,0:T(8,128)(2,1)} %pack.1), calls=%async_computation | async-start | bytes 2621440 | tf_op jit(solution)/shard_map/all_to_all | solution.py:450
  14.9 0.0 copy-start.3
  15.5 0.0 copy-done.4
  15.5 0.0 copy-done.2
  15.6 5.4 %sides.1 = (bf16[16,320,256]{2,1,0:T(8,128)(2,1)S(1)}, bf16[16,96,256]{2,1,0:T(8,128)(2,1)S(1)}, bf16[16,96,256]{2,1,0:T(8,128)(2,1)S(1)}, f32[8,128]{1,0:T(8,128)S(1)}) custom-call(s32[1]{0:T(128)} %bitcast.7.column_ref, bf16[64,2,96,96]{3,2,1,0:T(8,128)(2,1)} %vec_ref.1, bf16[2,96,96]{2,1,0:T(8,128)(2,1)S(1)} %copy-done.2, f32[1,1]{1,0:T(1,128)} %bitcast.16.fermi_ref), custom_call_target="tpu_custom_call" | custom-call | flops 1073741824 | bytes 5767168 | tf_op jit(solution)/shard_map/sides/pallas_call | solution.py:272
  20.9 0.0 copy-start
  21.0 1.5 %copy-done = bf16[16,320,256]{2,1,0:T(8,128)(2,1)} copy-done((bf16[16,320,256]{2,1,0:T(8,128)(2,1)}, bf16[16,320,256]{2,1,0:T(8,128)(2,1)S(1)}, u32[]{:S(2)}) %copy-start) | copy-done | bytes 2621464
  22.5 0.0 copy-done.3
  22.5 14.7 %all-to-all-done = bf16[128,8,640]{2,1,0:T(8,128)(2,1)S(1)} async-done(((bf16[128,8,640]{2,1,0:T(8,128)(2,1)}), bf16[128,8,640]{2,1,0:T(8,128)(2,1)S(1)}, u32[]{:S(2)}, u32[]{:S(2)}) %all-to-all-start) | async-done | bytes 1310752 | tf_op jit(solution)/shard_map/all_to_all | solution.py:450
  37.2 0.1 convert_bitcast_fusion
  37.3 0.1 copy.9
  37.4 8.3 %interpolate.1 = bf16[32,16,2304]{2,1,0:T(8,128)(2,1)S(1)} custom-call(f32[512,8]{1,0:T(8,128)S(1)} %bitcast.18, f32[8,1024]{1,0:T(8,128)S(1)} %pad_maximum_fusion.lat_ref, bf16[1024,640]{1,0:T(8,128)(2,1)S(1)} %bitcast.17), custom_call_target="tpu_custom_call" | custom-call | tf_op jit(solution)/shard_map/interpolate/pallas_call | solution.py:200
  45.8 0.0 copy-start.1
  45.8 34.8 %all_to_all.15.got_ref = bf16[32,16,2304]{2,1,0:T(8,128)(2,1)S(1)} all-to-all(bf16[32,16,2304]{2,1,0:T(8,128)(2,1)S(1)} %interpolate.1), channel_id=1, replica_groups=mesh['z'=4,'y'=4,'core'=2,'x'=4] {'y','core','x'}, dimensions={0} | all-to-all | bytes 4718592 | tf_op jit(solution)/shard_map/all_to_all | solution.py:450
  80.6 0.0 copy-done.1
  80.6 6.2 %bands.1 = (f32[9,16,96]{2,1,0:T(8,128)}, f32[128,8,128]{2,1,0:T(8,128)S(1)}) custom-call(bf16[16,320,256]{2,1,0:T(8,128)(2,1)S(1)} %copy-done.1, bf16[16,96,256]{2,1,0:T(8,128)(2,1)S(1)} %get-tuple-element.18.ut_ref, bf16[16,96,256]{2,1,0:T(8,128)(2,1)S(1)} %get-tuple-element.19.sb_ref, bf16[32,16,2304]{2,1,0:T(8,128)(2,1)S(1)} %all_to_all.15.got_ref, ...), custom_call_target="tpu_custom_call" | custom-call | tf_op jit(solution)/shard_map/bands/pallas_call | solution.py:410
  86.8 18.1 %all_to_all.16.parts_ref = f32[128,8,128]{2,1,0:T(8,128)} all-to-all(f32[128,8,128]{2,1,0:T(8,128)S(1)} %get-tuple-element.23), channel_id=1, replica_groups=mesh['z'=4,'y'=4,'core'=2,'x'=4] {'z','y','core','x'}, dimensions={0} | all-to-all | bytes 1048576 | tf_op jit(solution)/shard_map/all_to_all | solution.py:450
  104.9 1.9 %total_sums.1 = f32[9,96]{1,0:T(8,128)} custom-call(f32[128,8,128]{2,1,0:T(8,128)} %all_to_all.16.parts_ref), custom_call_target="tpu_custom_call" | custom-call | tf_op jit(solution)/shard_map/total_sums/pallas_call | solution.py:440
  (5 shorter events, 0.1 us)
Async XLA Ops:
  0.6 14.9 %copy-start.4 = (s32[1024]{0:T(1024)S(1)}, s32[1024]{0:T(1024)}, u32[]{:S(2)}) copy-start(s32[1024]{0:T(1024)} %param.12) | copy-start | bytes 12292
  0.6 14.9 %copy-start.2 = (bf16[2,96,96]{2,1,0:T(8,128)(2,1)S(1)}, bf16[2,96,96]{2,1,0:T(8,128)(2,1)}, u32[]{:S(2)}) copy-start(bf16[2,96,96]{2,1,0:T(8,128)(2,1)} %spin_ref.1) | copy-start | bytes 110596
  3.4 33.8 %all-to-all-start = ((bf16[128,8,640]{2,1,0:T(8,128)(2,1)}), bf16[128,8,640]{2,1,0:T(8,128)(2,1)S(1)}, u32[]{:S(2)}, u32[]{:S(2)}) async-start(bf16[128,8,640]{2,1,0:T(8,128)(2,1)} %pack.1), calls=%async_computation | async-start | bytes 2621440 | tf_op jit(solution)/shard_map/all_to_all | solution.py:450
  14.9 7.6 %copy-start.3 = (s32[1024,3]{0,1:T(4,128)S(1)}, s32[1024,3]{0,1:T(4,128)}, u32[]{:S(2)}) copy-start(s32[1024,3]{0,1:T(4,128)} %param.11) | copy-start | bytes 36868
  20.9 1.5 %copy-start = (bf16[16,320,256]{2,1,0:T(8,128)(2,1)}, bf16[16,320,256]{2,1,0:T(8,128)(2,1)S(1)}, u32[]{:S(2)}) copy-start(bf16[16,320,256]{2,1,0:T(8,128)(2,1)S(1)} %get-tuple-element.17.wu_ref) | copy-start | bytes 7864324
  45.8 34.8 %copy-start.1 = (bf16[16,320,256]{2,1,0:T(8,128)(2,1)S(1)}, bf16[16,320,256]{2,1,0:T(8,128)(2,1)}, u32[]{:S(2)}) copy-start(bf16[16,320,256]{2,1,0:T(8,128)(2,1)} %copy-done) | copy-start | bytes 7864324

commit v6 on v4

--- a/solution.py
+++ b/solution.py
@@ -172,12 +172,13 @@
         phase_block(k_ref[i * STEP_K : (i + 1) * STEP_K, :], lat_ref, p_refs[i % 2])
 
     phases(0)
-    turn_hopping(hop_ref, w_ref)
     for i in range(steps):
+        p_ref = p_refs[i % 2]
+        summed = jnp.dot(p_ref[:, 0:NR], hop_ref[...], preferred_element_type=f32)
+        if i == 0:
+            turn_hopping(hop_ref, w_ref)
         if i + 1 < steps:
             phases(i + 1)
-        p_ref = p_refs[i % 2]
-        summed = jnp.dot(p_ref[:, 0:NR], hop_ref[...], preferred_element_type=f32)
         summed += jnp.dot(p_ref[:, NR : 2 * NR], w_ref[...], preferred_element_type=f32)
         for pair in range(2):
             even = summed[2 * pair * STEP_K : (2 * pair + 1) * STEP_K]

time: 106 us -> 106 us (level)
  no operation moved by 1% of the time
where the time goes in v6:
time: 106 us
  blocking collectives  52.8 us (50%)
  Pallas kernels  22.6 us (21%)
  waiting for transfers between devices  14.7 us (14%)
  starting transfers between devices  11.5 us (11%)
  local copies, waits for them, and re-layouts  1.85 us (2%)
  between operations  1.41 us (1%)
    all_to_all x2, blocking collectives, exchange(): return lax.all_to_all(value, axes, split_axis=0, concat_axis=0, tiled=True)  52.8 us
    all_to_all x1, waiting for transfers between devices, exchange(): return lax.all_to_all(value, axes, split_axis=0, concat_axis=0, tiled=True)  14.7 us
    all_to_all x1, starting transfers between devices, exchange(): return lax.all_to_all(value, axes, split_axis=0, concat_axis=0, tiled=True)  11.5 us
    pallas_call x1, Pallas kernels, interpolate(): pl.pallas_call(interpolate_kernel, in_specs=[vmem, vmem, vmem], out_specs...  8.33 us
    pallas_call x1, Pallas kernels, bands(): pl.pallas_call(bands_kernel, in_specs=[vmem] * 5, out_specs=[vmem] * 2, o...  6.19 us
    pallas_call x1, Pallas kernels, sides(): pl.pallas_call(sides_kernel, grid_spec=grid_spec, out_shape=[jax.ShapeDty...  5.38 us
    pallas_call x1, Pallas kernels, pack(): pl.pallas_call(pack_kernel, in_specs=[vmem, vmem], out_specs=pl.BlockSpec...  2.72 us
  transfers between devices with their start and end apart: 1, of which 1 were waited for; matrix products, arithmetic and copies ran while one was open for 0% of the time, Pallas kernels for 5%

profile of v6, /device:TPU:1, one launch (start us, length us, event | category | flops | bytes accessed | tf_op | source)
XLA Modules:
  0.0 105.7 jit_solution(3425314016811072250)
XLA Ops:
  0.6 0.0 copy-start.4
  0.6 0.0 copy-start.2
  0.7 2.7 %pack.1 = bf16[128,8,640]{2,1,0:T(8,128)(2,1)} custom-call(bf16[8,2,9216]{2,1,0:T(2,128)(2,1)} %ham_ref.1, s32[3,64]{1,0:T(4,128)} %bitcast.22), custom_call_target="tpu_custom_call" | custom-call | tf_op jit(solution)/shard_map/pack/pallas_call | solution.py:121
  3.4 11.5 %all-to-all-start = ((bf16[128,8,640]{2,1,0:T(8,128)(2,1)}), bf16[128,8,640]{2,1,0:T(8,128)(2,1)S(1)}, u32[]{:S(2)}, u32[]{:S(2)}) async-start(bf16[128,8,640]{2,1,0:T(8,128)(2,1)} %pack.1), calls=%async_computation | async-start | bytes 2621440 | tf_op jit(solution)/shard_map/all_to_all | solution.py:428
  14.9 0.0 copy-start.3
  15.5 0.0 copy-done.4
  15.6 0.0 copy-done.2
  15.6 5.4 %sides.1 = (bf16[16,320,256]{2,1,0:T(8,128)(2,1)S(1)}, bf16[16,96,256]{2,1,0:T(8,128)(2,1)S(1)}, bf16[16,96,256]{2,1,0:T(8,128)(2,1)S(1)}, f32[8,128]{1,0:T(8,128)S(1)}) custom-call(s32[1]{0:T(128)} %bitcast.7.column_ref, bf16[64,2,96,96]{3,2,1,0:T(8,128)(2,1)} %vec_ref.1, bf16[2,96,96]{2,1,0:T(8,128)(2,1)S(1)} %copy-done.2, f32[1,1]{1,0:T(1,128)} %bitcast.17.fermi_ref), custom_call_target="tpu_custom_call" | custom-call | flops 1073741824 | bytes 5767168 | tf_op jit(solution)/shard_map/sides/pallas_call | solution.py:273
  21.0 0.0 copy-start
  21.0 1.5 %copy-done = bf16[16,320,256]{2,1,0:T(8,128)(2,1)} copy-done((bf16[16,320,256]{2,1,0:T(8,128)(2,1)}, bf16[16,320,256]{2,1,0:T(8,128)(2,1)S(1)}, u32[]{:S(2)}) %copy-start) | copy-done | bytes 2621464
  22.5 0.0 copy-done.3
  22.5 14.7 %all-to-all-done = bf16[128,8,640]{2,1,0:T(8,128)(2,1)S(1)} async-done(((bf16[128,8,640]{2,1,0:T(8,128)(2,1)}), bf16[128,8,640]{2,1,0:T(8,128)(2,1)S(1)}, u32[]{:S(2)}, u32[]{:S(2)}) %all-to-all-start) | async-done | bytes 1310752 | tf_op jit(solution)/shard_map/all_to_all | solution.py:428
  37.2 0.1 convert_bitcast_fusion
  37.3 0.1 copy.9
  37.5 8.3 %interpolate.1 = bf16[32,16,2304]{2,1,0:T(8,128)(2,1)S(1)} custom-call(f32[512,8]{1,0:T(8,128)S(1)} %bitcast.19, f32[8,1024]{1,0:T(8,128)S(1)} %pad_maximum_fusion.lat_ref, bf16[1024,640]{1,0:T(8,128)(2,1)S(1)} %bitcast.18), custom_call_target="tpu_custom_call" | custom-call | tf_op jit(solution)/shard_map/interpolate/pallas_call | solution.py:201
  45.8 0.0 copy-start.1
  45.8 34.8 %all_to_all.15.got_ref = bf16[32,16,2304]{2,1,0:T(8,128)(2,1)S(1)} all-to-all(bf16[32,16,2304]{2,1,0:T(8,128)(2,1)S(1)} %interpolate.1), channel_id=1, replica_groups=mesh['z'=4,'y'=4,'core'=2,'x'=4] {'y','core','x'}, dimensions={0} | all-to-all | bytes 4718592 | tf_op jit(solution)/shard_map/all_to_all | solution.py:428
  80.6 0.0 copy-done.1
  80.6 6.2 %bands.1 = (f32[9,16,96]{2,1,0:T(8,128)}, f32[128,8,128]{2,1,0:T(8,128)S(1)}) custom-call(bf16[16,320,256]{2,1,0:T(8,128)(2,1)S(1)} %copy-done.1, bf16[16,96,256]{2,1,0:T(8,128)(2,1)S(1)} %get-tuple-element.18.ut_ref, bf16[16,96,256]{2,1,0:T(8,128)(2,1)S(1)} %get-tuple-element.19.sb_ref, bf16[32,16,2304]{2,1,0:T(8,128)(2,1)S(1)} %all_to_all.15.got_ref, ...), custom_call_target="tpu_custom_call" | custom-call | tf_op jit(solution)/shard_map/bands/pallas_call | solution.py:411
  86.8 18.0 %all_to_all.16 = f32[128,8,128]{2,1,0:T(8,128)S(1)} all-to-all(f32[128,8,128]{2,1,0:T(8,128)S(1)} %get-tuple-element.23), channel_id=1, replica_groups=mesh['z'=4,'y'=4,'core'=2,'x'=4] {'z','y','core','x'}, dimensions={0} | all-to-all | bytes 1048576 | tf_op jit(solution)/shard_map/all_to_all | solution.py:428
  104.8 0.1 reduce_sum.9
  104.9 0.1 slice.11
  105.0 0.1 reshape.29
  105.1 0.6 pad_maximum_fusion.1
  (6 shorter events, 0.1 us)
Async XLA Ops:
  0.6 14.9 %copy-start.4 = (s32[1024]{0:T(1024)S(1)}, s32[1024]{0:T(1024)}, u32[]{:S(2)}) copy-start(s32[1024]{0:T(1024)} %param.12) | copy-start | bytes 12292
  0.6 14.9 %copy-start.2 = (bf16[2,96,96]{2,1,0:T(8,128)(2,1)S(1)}, bf16[2,96,96]{2,1,0:T(8,128)(2,1)}, u32[]{:S(2)}) copy-start(bf16[2,96,96]{2,1,0:T(8,128)(2,1)} %spin_ref.1) | copy-start | bytes 110596
  3.4 33.8 %all-to-all-start = ((bf16[128,8,640]{2,1,0:T(8,128)(2,1)}), bf16[128,8,640]{2,1,0:T(8,128)(2,1)S(1)}, u32[]{:S(2)}, u32[]{:S(2)}) async-start(bf16[128,8,640]{2,1,0:T(8,128)(2,1)} %pack.1), calls=%async_computation | async-start | bytes 2621440 | tf_op jit(solution)/shard_map/all_to_all | solution.py:428
  14.9 7.6 %copy-start.3 = (s32[1024,3]{0,1:T(4,128)S(1)}, s32[1024,3]{0,1:T(4,128)}, u32[]{:S(2)}) copy-start(s32[1024,3]{0,1:T(4,128)} %param.11) | copy-start | bytes 36868
  21.0 1.5 %copy-start = (bf16[16,320,256]{2,1,0:T(8,128)(2,1)}, bf16[16,320,256]{2,1,0:T(8,128)(2,1)S(1)}, u32[]{:S(2)}) copy-start(bf16[16,320,256]{2,1,0:T(8,128)(2,1)S(1)} %get-tuple-element.17.wu_ref) | copy-start | bytes 7864324
  45.8 34.8 %copy-start.1 = (bf16[16,320,256]{2,1,0:T(8,128)(2,1)S(1)}, bf16[16,320,256]{2,1,0:T(8,128)(2,1)}, u32[]{:S(2)}) copy-start(bf16[16,320,256]{2,1,0:T(8,128)(2,1)} %copy-done) | copy-start | bytes 7864324
